TPU v7x, 32 devices: a 4x4x1 block of a 4x4x8 slice. The times are simulated.
32 devices in a mesh: dp: 1 (over z), ep: 32 (over y, x, core).
Axes of the slice: x: 4, y: 4, z: 1, core: 2. Of those that a mesh axis runs over, the one named last changes fastest.
The devices are a block of a 4x4x8 slice.
Arguments:
- hidden_in: bfloat16 [1024, 2048], P(('dp', 'ep'))
- kv_cache: bfloat16 [1024, 256, 576], P(('dp', 'ep'))
- kv_lens: int32 [1024], P(('dp', 'ep'))
- routes: int32 [1024, 6], P(('dp', 'ep'))
- route_gates: float32 [1024, 6], P(('dp', 'ep'))
- w_q: bfloat16 [2048, 3072], replicated
- w_dkv: bfloat16 [2048, 576], replicated
- w_uk: bfloat16 [16, 128, 512], replicated
- w_uv: bfloat16 [16, 512, 128], replicated
- w_o: bfloat16 [2048, 2048], replicated
- sh_gate: bfloat16 [2048, 2816], replicated
- sh_up: bfloat16 [2048, 2816], replicated
- sh_down: bfloat16 [2816, 2048], replicated
- ex_gate: bfloat16 [64, 2048, 1408], P('ep')
- ex_up: bfloat16 [64, 2048, 1408], P('ep')
- ex_down: bfloat16 [64, 1408, 2048], P('ep')
Outputs:
- output 1: bfloat16 [1024, 2048], P(('dp', 'ep'))
- output 2: bfloat16 [1024, 576], P(('dp', 'ep'))
All inputs are finite; a program needn't handle non-finite values.
Results may differ from a plain program's by a relative error of at most 0.0158559.
Values are sent between devices in bfloat16 or wider.
A program may use at most 768 MiB of HBM per device.

v0:
```python
import jax
import jax.numpy as jnp
from jax import lax
from jax.sharding import PartitionSpec as P


def rotary(vec, cos_t, sin_t):
    half_dim = vec.shape[-1] // 2
    lead_part = vec[..., :half_dim]
    tail_part = vec[..., half_dim:]
    return jnp.concatenate([lead_part * cos_t - tail_part * sin_t, tail_part * cos_t + lead_part * sin_t], axis=-1)


def rotary_table(positions, rot_width):
    half_dim = rot_width // 2
    inv_freq = jnp.exp(jnp.arange(half_dim, dtype=jnp.float32) * (-2.0 * jnp.log(10000.0) / rot_width))
    angle_val = positions.astype(jnp.float32)[:, None] * inv_freq[None, :]
    return jnp.cos(angle_val), jnp.sin(angle_val)


def attend_local(x_blk, cache_blk, len_blk, w_q, w_dkv, w_uk, w_uv, w_o):
    num_seq = x_blk.shape[0]
    num_heads, nope_dim, latent = w_uk.shape
    rope_dim = cache_blk.shape[2] - latent
    v_dim = w_uv.shape[2]
    q_all = jnp.dot(x_blk, w_q, preferred_element_type=jnp.float32).astype(jnp.bfloat16).reshape(num_seq, num_heads, nope_dim + rope_dim)
    kv_raw = jnp.dot(x_blk, w_dkv, preferred_element_type=jnp.float32)
    cos_t, sin_t = rotary_table(len_blk, rope_dim)
    kv_row = jnp.concatenate([kv_raw[:, :latent], rotary(kv_raw[:, latent:], cos_t, sin_t)], axis=1).astype(jnp.bfloat16)
    q_rope = rotary(q_all[:, :, nope_dim:].astype(jnp.float32), cos_t[:, None, :], sin_t[:, None, :]).astype(jnp.bfloat16)
    q_lat = jnp.einsum("bhn,hnc->bhc", q_all[:, :, :nope_dim], w_uk, preferred_element_type=jnp.float32).astype(jnp.bfloat16)
    q_cat = jnp.concatenate([q_lat, q_rope], axis=2)
    score_scale = (nope_dim + rope_dim) ** -0.5
    s_old = jnp.einsum("bhc,blc->bhl", q_cat, cache_blk, preferred_element_type=jnp.float32) * score_scale
    s_new = jnp.einsum("bhc,bc->bh", q_cat, kv_row, preferred_element_type=jnp.float32) * score_scale
    valid_mask = jnp.arange(cache_blk.shape[1])[None, None, :] < len_blk[:, None, None]
    s_old = jnp.where(valid_mask, s_old, -jnp.inf)
    top_score = jnp.maximum(jnp.max(s_old, axis=2), s_new)
    e_old = jnp.exp(s_old - top_score[:, :, None])
    e_new = jnp.exp(s_new - top_score)
    denom_sum = jnp.sum(e_old, axis=2) + e_new
    p_old = (e_old / denom_sum[:, :, None]).astype(jnp.bfloat16)
    p_new = (e_new / denom_sum).astype(jnp.bfloat16)
    o_full = jnp.einsum("bhl,blc->bhc", p_old, cache_blk, preferred_element_type=jnp.float32) + p_new.astype(jnp.float32)[:, :, None] * kv_row.astype(jnp.float32)[:, None, :]
    o_lat = o_full[:, :, :latent].astype(jnp.bfloat16)
    v_head = jnp.einsum("bhc,hcv->bhv", o_lat, w_uv, preferred_element_type=jnp.float32).astype(jnp.bfloat16)
    attn_out = jnp.dot(v_head.reshape(num_seq, num_heads * v_dim), w_o, preferred_element_type=jnp.float32).astype(jnp.bfloat16)
    h_mid = (x_blk.astype(jnp.float32) + attn_out.astype(jnp.float32)).astype(jnp.bfloat16)
    return h_mid, kv_row


def swiglu(rows_in, w_gate, w_up, w_down):
    gate_val = jnp.dot(rows_in, w_gate, preferred_element_type=jnp.float32)
    up_val = jnp.dot(rows_in, w_up, preferred_element_type=jnp.float32)
    act_val = (jax.nn.silu(gate_val) * up_val).astype(jnp.bfloat16)
    return jnp.dot(act_val, w_down, preferred_element_type=jnp.float32).astype(jnp.bfloat16)


def expert_rows(row_buf, ex_gate, ex_up, ex_down):
    gate_val = jnp.einsum("gch,ghf->gcf", row_buf, ex_gate, preferred_element_type=jnp.float32)
    up_val = jnp.einsum("gch,ghf->gcf", row_buf, ex_up, preferred_element_type=jnp.float32)
    act_val = (jax.nn.silu(gate_val) * up_val).astype(jnp.bfloat16)
    return jnp.einsum("gcf,gfh->gch", act_val, ex_down, preferred_element_type=jnp.float32).astype(jnp.bfloat16)


def expert_cap(seqs_dev, top_k, group_size, local_exp):
    hot_devs = group_size // 4
    pair_cap = (seqs_dev * ((3 * top_k) // 4) + hot_devs - 1) // hot_devs
    return (pair_cap + local_exp - 1) // local_exp


def solution(mesh):
    group_size = mesh.shape["ep"]

    def device_step(x_blk, cache_blk, len_blk, routes, route_gates, w_q, w_dkv, w_uk, w_uv, w_o, sh_gate, sh_up, sh_down, ex_gate, ex_up, ex_down):
        num_seq, hidden = x_blk.shape
        top_k = routes.shape[1]
        local_exp = ex_gate.shape[0]
        num_exp = local_exp * group_size
        exp_cap = expert_cap(num_seq, top_k, group_size, local_exp)
        h_mid, kv_row = attend_local(x_blk, cache_blk, len_blk, w_q, w_dkv, w_uk, w_uv, w_o)
        shared = swiglu(h_mid, sh_gate, sh_up, sh_down)
        flat_ids = routes.reshape(-1)
        onehot = (flat_ids[:, None] == jnp.arange(num_exp, dtype=jnp.int32)[None, :]).astype(jnp.int32)
        rank_pos = jnp.sum((jnp.cumsum(onehot, axis=0) - onehot) * onehot, axis=1)
        slot_idx = (flat_ids % local_exp) * (group_size * exp_cap) + (flat_ids // local_exp) * exp_cap + rank_pos
        token_ids = jnp.arange(num_seq * top_k, dtype=jnp.int32) // top_k
        slot_token = jnp.zeros((num_exp * exp_cap,), jnp.int32).at[slot_idx].set(token_ids)
        send_buf = jnp.take(h_mid, slot_token, axis=0).reshape(local_exp, group_size, exp_cap, hidden)
        recv_buf = lax.all_to_all(send_buf, "ep", 1, 1, tiled=True)
        exp_out = expert_rows(recv_buf.reshape(local_exp, group_size * exp_cap, hidden), ex_gate, ex_up, ex_down)
        back_buf = lax.all_to_all(exp_out.reshape(local_exp, group_size, exp_cap, hidden), "ep", 1, 1, tiled=True)
        picked = jnp.take(back_buf.reshape(num_exp * exp_cap, hidden), slot_idx, axis=0).reshape(num_seq, top_k, hidden)
        routed = jnp.sum(picked.astype(jnp.float32) * route_gates[:, :, None], axis=1)
        layer_out = (h_mid.astype(jnp.float32) + shared.astype(jnp.float32) + routed).astype(jnp.bfloat16)
        return layer_out, kv_row

    batch_spec = P(("dp", "ep"))
    weight_spec = P()
    expert_spec = P("ep")
    in_specs = (batch_spec,) * 5 + (weight_spec,) * 8 + (expert_spec,) * 3
    return jax.shard_map(device_step, mesh=mesh, in_specs=in_specs, out_specs=(batch_spec, batch_spec), check_vma=False)
```

profile of v0, /device:TPU:97, one launch (start us, length us, event | category | flops | bytes accessed | tf_op | source)
XLA Modules:
  0.0 140.8 jit_solution(14417251250629118873)
XLA Ops:
  0.7 7.1 %convolution_convert_fusion = bf16[32,3072]{1,0:T(8,128)(2,1)S(1)} fusion(bf16[32,2048]{1,0:T(8,128)(2,1)} %param.16, bf16[2048,3072]{1,0:T(8,128)(2,1)} %param.21), kind=kOutput, calls=%fused_computation.6 | convolution fusion | flops 402751488 | bytes 12910592 | tf_op jit(solution)/shard_map/dot_general | solution.py:26
  7.8 0.3 reshape.280
  8.2 0.8 fusion.56
  9.0 0.1 subtract_convert_fusion.1
  9.7 0.6 reduce-window.6
  10.3 0.2 slice_reduce_fusion
  10.7 1.2 scatter_custom_fusion
  12.0 2.0 %fusion.15 = bf16[32,16,512]{2,0,1:T(8,128)(2,1)S(1)} fusion(bf16[16,128,512]{2,1,0:T(8,128)(2,1)} %param.23, bf16[32,16,128]{2,1,0:T(8,128)(2,1)S(1)} %slice.53), kind=kOutput, calls=%fused_computation.27 | convolution fusion | flops 67371008 | bytes 2752512 | tf_op jit(solution)/shard_map/bhn,hnc->bhc/dot_general | solution.py:31
  14.0 0.1 subtract_convert_fusion
  14.3 0.4 fusion.19
  14.6 5.4 %fusion.55 = (f32[32,16]{1,0:T(8,128)S(1)}, f32[32,16,256]{2,1,0:T(8,128)S(1)}) fusion(bf16[32,256,576]{1,2,0:T(8,128)(2,1)} %param.17, bf16[32,16,576]{2,0,1:T(8,128)(2,1)S(1)} %pad_maximum_fusion, pred[32,256]{1,0:T(8,128)(4,1)S(1)} %iota_compare_fusion.2), kind=kOutput, calls=%fused_computation.117 | convolution fusion | flops 151387648 | bytes 10561536 | tf_op jit(solution)/shard_map/bhc,blc->bhl/dot_general | solution.py:34
  20.1 0.3 fusion.23
  20.5 0.2 slice-done.2
  20.7 2.6 %fusion.29 = f32[32,16,576]{2,1,0:T(8,128)S(1)} fusion(bf16[32,256,576]{1,2,0:T(8,128)(2,1)S(1)} %bitcast.54, f32[32,16,256]{2,1,0:T(8,128)S(1)} %get-tuple-element.11, f32[32,16]{1,0:T(8,128)S(1)} %get-tuple-element.7, f32[32,16]{1,0:T(8,128)S(1)} %multiply_maximum_fusion), kind=kOutput, calls=%fused_computation.47 | convolution fusion | flops 151388160 | bytes 11145216 | tf_op jit(solution)/shard_map/bhl,blc->bhc/dot_general | solution.py:44
  23.5 0.2 fusion.18
  23.6 2.2 %fusion.17 = bf16[16,4,8,128]{3,2,1,0:T(8,128)(2,1)S(1)} fusion(bf16[16,512,128]{2,1,0:T(8,128)(2,1)} %param.24, bf16[32,16,512]{2,1,0:T(8,128)(2,1)S(1)} %fusion.18), kind=kOutput, calls=%fused_computation.31 | convolution fusion | flops 67174400 | bytes 2752512 | tf_op jit(solution)/shard_map/bhc,hcv->bhv/dot_general | solution.py:46
  25.8 4.9 %fusion.9 = bf16[32,2048]{1,0:T(8,128)(2,1)S(1)} fusion(bf16[2048,2048]{1,0:T(8,128)(2,1)} %param.25, bf16[32,2048]{1,0:T(8,128)(2,1)S(1)} %copy-done.2, bf16[16,4,8,128]{3,2,1,0:T(8,128)(2,1)S(1)} %fusion.17), kind=kOutput, calls=%fused_computation.18 | convolution fusion | flops 268763136 | bytes 8781824 | tf_op jit(solution)/shard_map/dot_general | solution.py:47
  30.7 2.5 %gather_fusion = bf16[512,2048]{1,0:T(8,128)(2,1)S(1)} fusion(bf16[32,2048]{1,0:T(8,128)(2,1)S(1)} %fusion.9, s32[1024]{0:T(1024)S(1)} %pad_clamp_fusion.1), kind=kCustom, calls=%fused_computation | custom fusion | bytes 4196352 | tf_op jit(solution)/shard_map/jit(_take)/gather | solution.py:89
  33.2 0.3 copy_select_fusion
  33.5 38.7 %all_to_all.10 = bf16[2,32,8,2048]{3,2,0,1:T(8,128)(2,1)S(1)} all-to-all(bf16[2,32,8,2048]{3,2,0,1:T(8,128)(2,1)S(1)} %copy_select_fusion), channel_id=1, replica_groups=mesh['dp'=1,'ep'=32] {'ep'}, dimensions={1} | all-to-all | bytes 4194304 | tf_op jit(solution)/shard_map/all_to_all | solution.py:90
  72.2 9.4 %fusion.11 = f32[2,256,1408]{2,1,0:T(8,128)} fusion(bf16[2,2048,1408]{2,1,0:T(8,128)(2,1)} %param.29, bf16[2,32,8,2048]{3,2,0,1:T(8,128)(2,1)S(1)} %all_to_all.10), kind=kOutput, calls=%fused_computation.20 | convolution fusion | flops 2952790016 | bytes 16515072 | tf_op jit(solution)/shard_map/gch,ghf->gcf/dot_general | solution.py:60
  81.7 5.3 %fusion.1 = bf16[2,256,1408]{2,1,0:T(8,128)(2,1)S(1)} fusion(bf16[2,2048,1408]{2,1,0:T(8,128)(2,1)S(1)} %bitcast.63, f32[2,256,1408]{2,1,0:T(8,128)} %fusion.11, bf16[2,32,8,2048]{3,2,0,1:T(8,128)(2,1)S(1)} %all_to_all.10), kind=kOutput, calls=%fused_computation.7 | convolution fusion | flops 2957115392 | bytes 17956864 | tf_op jit(solution)/shard_map/gch,ghf->gcf/dot_general | solution.py:61
  87.0 3.6 %fusion.2 = bf16[2,32,8,2048]{3,2,1,0:T(8,128)(2,1)S(1)} fusion(bf16[2,256,1408]{2,1,0:T(8,128)(2,1)S(1)} %fusion.1, bf16[2,1408,2048]{2,1,0:T(8,128)(2,1)S(1)} %bitcast.65), kind=kOutput, calls=%fused_computation.9 | convolution fusion | flops 2953838592 | bytes 15073280 | tf_op jit(solution)/shard_map/gcf,gfh->gch/dot_general | solution.py:63
  90.7 1.6 %copy.54 = bf16[2,32,8,2048]{3,2,0,1:T(8,128)(2,1)} copy(bf16[2,32,8,2048]{3,2,1,0:T(8,128)(2,1)S(1)} %fusion.2) | data formatting | bytes 4194304 | tf_op jit(solution)/shard_map/reshape | solution.py:92
  92.2 4.0 %all-to-all-start.1 = ((bf16[2,32,8,2048]{3,2,0,1:T(8,128)(2,1)}), bf16[2,32,8,2048]{3,2,0,1:T(8,128)(2,1)}, u32[]{:S(2)}, u32[]{:S(2)}) async-start(bf16[2,32,8,2048]{3,2,0,1:T(8,128)(2,1)} %copy.54), calls=%async_computation.1 | async-start | bytes 4194304 | tf_op jit(solution)/shard_map/all_to_all | solution.py:92
  96.5 7.1 %fusion.57 = f32[32,2816]{1,0:T(8,128)} fusion(bf16[32,2048]{1,0:T(8,128)(2,1)S(1)} %fusion.9, bf16[2048,2816]{1,0:T(8,128)(2,1)} %param.26), kind=kOutput, calls=%fused_computation.119 | convolution fusion | flops 369098752 | bytes 12025856 | tf_op jit(solution)/shard_map/dot_general | solution.py:53
  103.6 19.9 %all-to-all-done.1 = bf16[2,32,8,2048]{3,2,0,1:T(8,128)(2,1)} async-done(((bf16[2,32,8,2048]{3,2,0,1:T(8,128)(2,1)}), bf16[2,32,8,2048]{3,2,0,1:T(8,128)(2,1)}, u32[]{:S(2)}, u32[]{:S(2)}) %all-to-all-start.1) | async-done | bytes 2097184 | tf_op jit(solution)/shard_map/all_to_all | solution.py:92
  123.4 1.8 %copy.55 = bf16[2,32,8,2048]{3,2,1,0:T(8,128)(2,1)S(1)} copy(bf16[2,32,8,2048]{3,2,0,1:T(8,128)(2,1)} %all-to-all-done.1) | data formatting | bytes 4194304 | tf_op jit(solution)/shard_map/all_to_all | solution.py:92
  125.3 1.2 gather_fusion.1
  126.4 0.3 gather.15
  126.7 1.6 %multiply_reduce_fusion = f32[32,2048]{1,0:T(8,128)S(1)} fusion(f32[32,6]{1,0:T(8,128)S(1)} %copy.56, bf16[32,6,2048]{2,1,0:T(8,128)(2,1)S(1)} %gather.15, pred[32,6]{1,0:T(8,128)(4,1)S(1)} %compare_and_fusion), kind=kLoop, calls=%fused_computation.23 | loop fusion | flops 1507328 | bytes 1049536 | tf_op jit(solution)/shard_map/reduce_sum | solution.py:94
  128.3 12.5 %fusion.6 = bf16[32,2048]{1,0:T(8,128)(2,1)} fusion(f32[32,2048]{1,0:T(8,128)S(1)} %multiply_reduce_fusion, bf16[2816,2048]{1,0:T(8,128)(2,1)} %param.28, bf16[32,2048]{1,0:T(8,128)(2,1)S(1)} %fusion.9, bf16[2048,2816]{1,0:T(8,128)(2,1)} %param.27, f32[32,2816]{1,0:T(8,128)} %fusion.57), kind=kOutput, calls=%fused_computation.14 | convolution fusion | flops 739131392 | bytes 23953408 | tf_op jit(solution)/shard_map/dot_general | solution.py:56
  (67 shorter events, 1.6 us)
Async XLA Ops:
  0.6 7.6 %copy-start = (bf16[2048,576]{0,1:T(8,128)(2,1)S(1)}, bf16[2048,576]{0,1:T(8,128)(2,1)}, u32[]{:S(2)}) copy-start(bf16[2048,576]{0,1:T(8,128)(2,1)} %param.22) | copy-start | bytes 7077892
  0.7 7.5 %copy-start.6 = (s32[32]{0:T(128)S(1)}, s32[32]{0:T(128)}, u32[]{:S(2)}) copy-start(s32[32]{0:T(128)} %param.18) | copy-start | bytes 388
  0.7 7.6 %copy-start.2 = (bf16[32,2048]{1,0:T(8,128)(2,1)S(1)}, bf16[32,2048]{1,0:T(8,128)(2,1)}, u32[]{:S(2)}) copy-start(bf16[32,2048]{1,0:T(8,128)(2,1)} %param.16) | copy-start | bytes 393220
  7.7 1.6 %copy-start.4 = (s32[32,6]{0,1:T(8,128)S(1)}, s32[32,6]{0,1:T(8,128)}, u32[]{:S(2)}) copy-start(s32[32,6]{0,1:T(8,128)} %param.19) | copy-start | bytes 2308
  9.3 13.9 %copy-start.3 = (bf16[32,576]{1,0:T(8,128)(2,1)}, bf16[32,576]{1,0:T(8,128)(2,1)S(1)}, u32[]{:S(2)}) copy-start(bf16[32,576]{1,0:T(8,128)(2,1)S(1)} %pad_maximum_fusion.1) | copy-start | bytes 110596
  14.3 6.1 %slice-start = ((s8[9437184]{0:T(1024)(128)(4,1)}), s8[4194304]{0:T(1024)(128)(4,1)S(1)}, s32[]{:S(2)}) async-start(s8[9437184]{0:T(1024)(128)(4,1)} %bitcast.53), calls=%async_computation.2 | async-start | bytes 8388608
  14.6 5.9 %slice-start.1 = ((s8[9437184]{0:T(1024)(128)(4,1)}), s8[4194304]{0:T(1024)(128)(4,1)S(1)}, s32[]{:S(2)}) async-start(s8[9437184]{0:T(1024)(128)(4,1)} %bitcast.53), calls=%async_computation.3 | async-start | bytes 8388608
  14.6 6.1 %slice-start.2 = ((s8[9437184]{0:T(1024)(128)(4,1)}), s8[1048576]{0:T(1024)(128)(4,1)S(1)}, s32[]{:S(2)}) async-start(s8[9437184]{0:T(1024)(128)(4,1)} %bitcast.53), calls=%async_computation.4 | async-start | bytes 2097152
  33.5 48.1 %slice-start.3 = ((s8[11534336]{0:T(1024)(128)(4,1)}), s8[4194304]{0:T(1024)(128)(4,1)S(1)}, s32[]{:S(2)}) async-start(s8[11534336]{0:T(1024)(128)(4,1)} %bitcast.62), calls=%async_computation.5 | async-start | bytes 8388608
  72.2 9.5 %slice-start.4 = ((s8[11534336]{0:T(1024)(128)(4,1)}), s8[4194304]{0:T(1024)(128)(4,1)S(1)}, s32[]{:S(2)}) async-start(s8[11534336]{0:T(1024)(128)(4,1)} %bitcast.62), calls=%async_computation.6 | async-start | bytes 8388608
  72.2 9.5 %slice-start.5 = ((s8[11534336]{0:T(1024)(128)(4,1)}), s8[3145728]{0:T(1024)(128)(4,1)S(1)}, s32[]{:S(2)}) async-start(s8[11534336]{0:T(1024)(128)(4,1)} %bitcast.62), calls=%async_computation.7 | async-start | bytes 6291456
  72.2 14.8 %slice-start.6 = ((s8[11534336]{0:T(1024)(128)(4,1)}), s8[4194304]{0:T(1024)(128)(4,1)S(1)}, s32[]{:S(2)}) async-start(s8[11534336]{0:T(1024)(128)(4,1)} %bitcast.64), calls=%async_computation.8 | async-start | bytes 8388608
  72.2 14.8 %slice-start.7 = ((s8[11534336]{0:T(1024)(128)(4,1)}), s8[4194304]{0:T(1024)(128)(4,1)S(1)}, s32[]{:S(2)}) async-start(s8[11534336]{0:T(1024)(128)(4,1)} %bitcast.64), calls=%async_computation.9 | async-start | bytes 8388608
  81.7 5.4 %slice-start.8 = ((s8[11534336]{0:T(1024)(128)(4,1)}), s8[3145728]{0:T(1024)(128)(4,1)S(1)}, s32[]{:S(2)}) async-start(s8[11534336]{0:T(1024)(128)(4,1)} %bitcast.64), calls=%async_computation.10 | async-start | bytes 6291456
  92.2 4.1 %copy-start.5 = (f32[32,6]{0,1:T(8,128)S(1)}, f32[32,6]{0,1:T(8,128)}, u32[]{:S(2)}) copy-start(f32[32,6]{0,1:T(8,128)} %param.20) | copy-start | bytes 2308
  92.2 31.2 %all-to-all-start.1 = ((bf16[2,32,8,2048]{3,2,0,1:T(8,128)(2,1)}), bf16[2,32,8,2048]{3,2,0,1:T(8,128)(2,1)}, u32[]{:S(2)}, u32[]{:S(2)}) async-start(bf16[2,32,8,2048]{3,2,0,1:T(8,128)(2,1)} %copy.54), calls=%async_computation.1 | async-start | bytes 4194304 | tf_op jit(solution)/shard_map/all_to_all | solution.py:92
  128.3 12.5 %copy-start.1 = (bf16[2048,576]{0,1:T(8,128)(2,1)S(1)}, bf16[2048,576]{0,1:T(8,128)(2,1)}, u32[]{:S(2)}) copy-start(bf16[2048,576]{0,1:T(8,128)(2,1)} %param.22) | copy-start | bytes 7077892
where the time goes:
time: 142 us; the launch traced here: 141 us
  matrix products  63.3 us (45%)
  blocking collectives  38.7 us (27%)
  waiting for transfers between devices  19.9 us (14%)
  local copies, waits for them, and re-layouts  10.1 us (7%)
  starting transfers between devices  4.02 us (3%)
  other arithmetic  3.85 us (3%)
    all_to_all x1, blocking collectives, device_step(): recv_buf = lax.all_to_all(send_buf, 'ep', 1, 1, tiled=True)  38.7 us
    all_to_all x1, waiting for transfers between devices, device_step(): lax.all_to_all(exp_out.reshape(local_exp, group_size, exp_cap, hidden), '...  19.9 us
    dot_general x1, matrix products, swiglu(): jnp.dot(act_val, w_down, preferred_element_type=jnp.float32)  12.5 us
    dot_general x1, matrix products, expert_rows(): jnp.einsum('gch,ghf->gcf', row_buf, ex_gate, preferred_element_type=jnp.f...  9.44 us
    dot_general x1, matrix products, swiglu(): gate_val = jnp.dot(rows_in, w_gate, preferred_element_type=jnp.float32)  7.07 us
    dot_general x1, matrix products, attend_local(): jnp.dot(x_blk, w_q, preferred_element_type=jnp.float32).astype(jnp.bfloat16)  7.05 us
    dot_general x1, matrix products, attend_local(): jnp.einsum('bhc,blc->bhl', q_cat, cache_blk, preferred_element_type=jnp.f...  5.44 us
    dot_general x1, matrix products, expert_rows(): jnp.einsum('gch,ghf->gcf', row_buf, ex_up, preferred_element_type=jnp.flo...  5.33 us
  transfers between devices with their start and end apart: 1, of which 1 were waited for; matrix products, arithmetic and copies ran while one was open for 5% of the time, Pallas kernels for 0%

commit v1 on v0

v1 whole, which is shorter than its diff:
```python
import functools

import jax
import jax.numpy as jnp
from jax import lax
from jax.experimental import pallas as pl
from jax.experimental.pallas import tpu as pltpu
from jax.sharding import PartitionSpec as P

MESH = pl.DeviceIdType.MESH
SLOTS_EXP = 8
LANES = 128

def rotary(vec, cos_t, sin_t):
    half_dim = vec.shape[-1] // 2
    lead_part = vec[..., :half_dim]
    tail_part = vec[..., half_dim:]
    return jnp.concatenate([lead_part * cos_t - tail_part * sin_t, tail_part * cos_t + lead_part * sin_t], axis=-1)


def rotary_table(positions, rot_width):
    half_dim = rot_width // 2
    inv_freq = jnp.exp(jnp.arange(half_dim, dtype=jnp.float32) * (-2.0 * jnp.log(10000.0) / rot_width))
    angle_val = positions.astype(jnp.float32)[:, None] * inv_freq[None, :]
    return jnp.cos(angle_val), jnp.sin(angle_val)


def attend_local(x_blk, cache_blk, len_blk, w_q, w_dkv, w_uk, w_uv, w_o):
    num_seq = x_blk.shape[0]
    num_heads, nope_dim, latent = w_uk.shape
    rope_dim = cache_blk.shape[2] - latent
    v_dim = w_uv.shape[2]
    q_all = jnp.dot(x_blk, w_q, preferred_element_type=jnp.float32).astype(jnp.bfloat16).reshape(num_seq, num_heads, nope_dim + rope_dim)
    kv_raw = jnp.dot(x_blk, w_dkv, preferred_element_type=jnp.float32)
    cos_t, sin_t = rotary_table(len_blk, rope_dim)
    kv_row = jnp.concatenate([kv_raw[:, :latent], rotary(kv_raw[:, latent:], cos_t, sin_t)], axis=1).astype(jnp.bfloat16)
    q_rope = rotary(q_all[:, :, nope_dim:].astype(jnp.float32), cos_t[:, None, :], sin_t[:, None, :]).astype(jnp.bfloat16)
    q_lat = jnp.einsum("bhn,hnc->bhc", q_all[:, :, :nope_dim], w_uk, preferred_element_type=jnp.float32).astype(jnp.bfloat16)
    q_cat = jnp.concatenate([q_lat, q_rope], axis=2)
    score_scale = (nope_dim + rope_dim) ** -0.5
    s_old = jnp.einsum("bhc,blc->bhl", q_cat, cache_blk, preferred_element_type=jnp.float32) * score_scale
    s_new = jnp.einsum("bhc,bc->bh", q_cat, kv_row, preferred_element_type=jnp.float32) * score_scale
    valid_mask = jnp.arange(cache_blk.shape[1])[None, None, :] < len_blk[:, None, None]
    s_old = jnp.where(valid_mask, s_old, -jnp.inf)
    top_score = jnp.maximum(jnp.max(s_old, axis=2), s_new)
    e_old = jnp.exp(s_old - top_score[:, :, None])
    e_new = jnp.exp(s_new - top_score)
    denom_sum = jnp.sum(e_old, axis=2) + e_new
    p_old = (e_old / denom_sum[:, :, None]).astype(jnp.bfloat16)
    p_new = (e_new / denom_sum).astype(jnp.bfloat16)
    o_full = jnp.einsum("bhl,blc->bhc", p_old, cache_blk, preferred_element_type=jnp.float32) + p_new.astype(jnp.float32)[:, :, None] * kv_row.astype(jnp.float32)[:, None, :]
    o_lat = o_full[:, :, :latent].astype(jnp.bfloat16)
    v_head = jnp.einsum("bhc,hcv->bhv", o_lat, w_uv, preferred_element_type=jnp.float32).astype(jnp.bfloat16)
    attn_out = jnp.dot(v_head.reshape(num_seq, num_heads * v_dim), w_o, preferred_element_type=jnp.float32).astype(jnp.bfloat16)
    h_mid = (x_blk.astype(jnp.float32) + attn_out.astype(jnp.float32)).astype(jnp.bfloat16)
    return h_mid, kv_row


def chip_order(side):
    def hops(off):
        return sum(min(v, side - v) for v in off)

    offs = [(dx, dy) for dy in range(side) for dx in range(side)]
    return sorted(offs, key=lambda off: (hops(off), -max(min(v, side - v) for v in off), off))


def moe_kernel(n_dev, h_ref, oh_ref, gate_ref, shg_hbm, shu_hbm, shd_hbm, exg_hbm, exu_hbm, exd_hbm, out_ref,
               h_all, oh_all, rows, act, y_buf, back, wg, wu, wd, ring_g, ring_u, ring_d, sh_acc,
               ag_send, ag_recv, core_send, core_recv, oh_send_sem, oh_recv_sem, ret_send, ret_recv, w_sem, ring_sem, local_sem):
    side = int((n_dev // 2) ** 0.5)
    offs = chip_order(side)
    slot_of = {off: k for k, off in enumerate(offs)}
    n_chips = len(offs)
    me = lax.axis_index("ep")
    core = lax.rem(me, 2)
    my_x = lax.rem(me // 2, side)
    my_y = me // (2 * side)
    hidden = h_ref.shape[1]
    q4 = hidden // 4

    def device_at(off, c):
        return (lax.rem(my_y + off[1], side) * side + lax.rem(my_x + off[0], side)) * 2 + c

    def minus(a, b):
        return ((a[0] - b[0]) % side, (a[1] - b[1]) % side)

    partner = device_at((0, 0), 1 - core)

    n_exp = wg.shape[0]
    w_copies = []
    for e in range(n_exp):
        for m, (src, dst) in enumerate(((exg_hbm, wg), (exu_hbm, wu), (exd_hbm, wd))):
            cp = pltpu.make_async_copy(src.at[e], dst.at[e], w_sem.at[e * 3 + m])
            cp.start()
            w_copies.append(cp)
    n_ring, _, blk = ring_g.shape
    n_steps = shg_hbm.shape[1] // blk

    def ring_copies(step, slot):
        cols = pl.ds(pl.multiple_of(step * blk, blk), blk)
        return (pltpu.make_async_copy(shg_hbm.at[:, cols], ring_g.at[slot], ring_sem.at[0, slot]),
                pltpu.make_async_copy(shu_hbm.at[:, cols], ring_u.at[slot], ring_sem.at[1, slot]),
                pltpu.make_async_copy(shd_hbm.at[cols, :], ring_d.at[slot], ring_sem.at[2, slot]))

    for s in range(n_ring):
        for cp in ring_copies(s, s):
            cp.start()

    h_all[core] = h_ref[...]
    oh_all[core] = oh_ref[0, core]

    barrier = pltpu.get_barrier_semaphore()
    for i in range(1, n_dev):
        pl.semaphore_signal(barrier, inc=1, device_id={"ep": lax.rem(me + i, n_dev)}, device_id_type=MESH)
    pl.semaphore_wait(barrier, n_dev - 1)

    A, B = (0, 2), (2, 2)
    A1, A0, B0, B1 = (0, 1), (1, 1), (2, 1), (3, 1)
    xp, xm, yp, ym = (1, 0), (side - 1, 0), (0, 1), (0, side - 1)
    pieces, sends, core_pieces = {}, [], {}

    def cols_of(part):
        return pl.ds(part[0] * q4, part[1] * q4)

    def forward(off, part, d):
        dst_off = minus(off, d)
        n = len(pieces)
        src = h_ref if off == (0, 0) else h_all.at[slot_of[off] * 2 + core]
        cp = pltpu.make_async_remote_copy(
            src_ref=src.at[:, cols_of(part)], dst_ref=h_all.at[slot_of[dst_off] * 2 + core, :, cols_of(part)],
            send_sem=ag_send.at[n], recv_sem=ag_recv.at[n], device_id={"ep": device_at(d, core)}, device_id_type=MESH)
        cp.start()
        pieces[(dst_off, part)] = cp
        sends.append(cp)

    def to_partner(off, part):
        n = len(core_pieces)
        src = h_ref if off == (0, 0) else h_all.at[slot_of[off] * 2 + core]
        cp = pltpu.make_async_remote_copy(
            src_ref=src.at[:, cols_of(part)], dst_ref=h_all.at[slot_of[off] * 2 + core, :, cols_of(part)],
            send_sem=core_send.at[n], recv_sem=core_recv.at[n], device_id={"ep": partner}, device_id_type=MESH)
        cp.start()
        core_pieces[(off, part)] = cp
        sends.append(cp)

    def arrived(off, *parts):
        for part in parts:
            pieces[(off, part)].wait_recv()

    for d in (xp, xm):
        forward((0, 0), A, d)
    for d in (yp, ym):
        forward((0, 0), B, d)
    for d in (xp, xm):
        forward((0, 0), B, d)
    for d in (yp, ym):
        forward((0, 0), A, d)
    to_partner((0, 0), A)
    to_partner((0, 0), B)

    oh_copies = []
    for k, off in enumerate(offs):
        there = slot_of[minus((0, 0), off)]
        for c in ((None,) if k == 0 else (0, 1)):
            dst_core = 1 - core if c is None else c
            n = len(oh_copies)
            cp = pltpu.make_async_remote_copy(
                src_ref=oh_ref.at[there % 2, k * 2 + dst_core], dst_ref=oh_all.at[there * 2 + core],
                send_sem=oh_send_sem.at[n], recv_sem=oh_recv_sem.at[there * 2 + core],
                device_id={"ep": device_at(off, dst_core)}, device_id_type=MESH)
            cp.start()
            oh_copies.append(cp)
            sends.append(cp)

    for off, d, quarter in ((xm, xp, A0), (xp, xm, A1)):
        arrived(off, A)
        forward(off, A, yp)
        forward(off, A, ym)
        forward(off, quarter, d)
        to_partner(off, A)
    for off, d, quarter in ((ym, yp, B0), (yp, ym, B1)):
        arrived(off, B)
        forward(off, B, xp)
        forward(off, B, xm)
        forward(off, quarter, d)
        to_partner(off, B)
    for off, d, quarter in ((xm, xp, B0), (xp, xm, B1)):
        arrived(off, B)
        forward(off, quarter, d)
        to_partner(off, B)
    for off, d, quarter in ((ym, yp, A0), (yp, ym, A1)):
        arrived(off, A)
        forward(off, quarter, d)
        to_partner(off, A)
    x2, y2 = (2, 0), (0, 2)
    arrived(x2, A0, A1)
    forward(x2, A, yp)
    forward(x2, A, ym)
    to_partner(x2, A)
    arrived(y2, B0, B1)
    forward(y2, B, xp)
    forward(y2, B, xm)
    to_partner(y2, B)
    diagonals = [(dx, dy) for dy in (1, side - 1) for dx in (1, side - 1)]
    for off in diagonals:
        arrived(off, A)
        if off[1] == 1:
            forward(off, A1, ym)
        else:
            forward(off, A0, yp)
        to_partner(off, A)
        arrived(off, B)
        if off[0] == 1:
            forward(off, B1, xm)
        else:
            forward(off, B0, xp)
        to_partner(off, B)
    arrived(x2, B0, B1)
    to_partner(x2, B)
    arrived(y2, A0, A1)
    to_partner(y2, A)

    def hop3():
        for off, d, quarter in (((2, side - 1), yp, A0), ((2, 1), ym, A1)):
            arrived(off, A)
            forward(off, quarter, d)
            to_partner(off, A)
        for off, d, quarter in (((side - 1, 2), xp, B0), ((1, 2), xm, B1)):
            arrived(off, B)
            forward(off, quarter, d)
            to_partner(off, B)
        for off in ((2, side - 1), (2, 1)):
            arrived(off, B0, B1)
            to_partner(off, B)
        for off in ((side - 1, 2), (1, 2)):
            arrived(off, A0, A1)
            to_partner(off, A)

    def hop4():
        far = (2, 2)
        arrived(far, A0, A1)
        to_partner(far, A)
        arrived(far, B0, B1)
        to_partner(far, B)

    def ready(ks):
        for k in ks:
            for part in (A, B):
                core_pieces[(offs[k], part)].wait_recv()
            for c in ((1 - core,) if k == 0 else (0, 1)):
                pltpu.make_async_remote_copy(
                    src_ref=oh_ref.at[0, 0], dst_ref=oh_all.at[k * 2 + c], send_sem=oh_send_sem.at[0],
                    recv_sem=oh_recv_sem.at[k * 2 + c], device_id={"ep": partner}, device_id_type=MESH).wait_recv()

    half = n_chips // 2
    n_src = half * 2
    n_row = n_src * SLOTS_EXP
    seqs = h_ref.shape[0]
    ff = wg.shape[2]

    def gather_rows(k0):
        def body(g, carry):
            s0 = k0 * 2 + g * 4
            table = oh_all[pl.ds(s0, 4)].reshape(4 * 2 * SLOTS_EXP, LANES)
            toks = h_all.at[pl.ds(s0, 4)]
            for j in range(hidden // 512):
                got = jnp.dot(table, toks[:, :, j * 512:(j + 1) * 512].reshape(4 * seqs, 512), preferred_element_type=jnp.float32)
                got = got.reshape(4, n_exp, SLOTS_EXP, 512)
                for e in range(n_exp):
                    rows[e, pl.ds(pl.multiple_of(g * 4 * SLOTS_EXP, 4 * SLOTS_EXP), 4 * SLOTS_EXP), j * 512:(j + 1) * 512] = (
                        got[:, e].reshape(4 * SLOTS_EXP, 512).astype(jnp.bfloat16))
            return carry

        lax.fori_loop(0, half // 2, body, 0)

    def gate_up(e):
        r = rows.at[e]
        full = ff // 256
        for j in range(full):
            cs = slice(j * 256, (j + 1) * 256)
            g = jnp.dot(r[...], wg[e, :, cs], preferred_element_type=jnp.float32)
            u = jnp.dot(r[...], wu[e, :, cs], preferred_element_type=jnp.float32)
            act[e, :, cs] = (jax.nn.silu(g) * u).astype(jnp.bfloat16)
        if ff % 256:
            cs = slice(full * 256, ff)
            wid = ff - full * 256
            both = jnp.dot(r[...], jnp.concatenate([wg[e, :, cs], wu[e, :, cs]], axis=1), preferred_element_type=jnp.float32)
            act[e, :, cs] = (jax.nn.silu(both[:, :wid]) * both[:, wid:]).astype(jnp.bfloat16)

    def down(k0):
        for j in range(hidden // 256):
            cs = slice(j * 256, (j + 1) * 256)
            outs = [jnp.dot(act[e], wd[e, :, cs], preferred_element_type=jnp.float32).reshape(n_src, 1, SLOTS_EXP, 256) for e in range(n_exp)]
            y_buf[k0 * 2:k0 * 2 + n_src, :, cs] = jnp.concatenate(outs, axis=1).reshape(n_src, n_exp * SLOTS_EXP, 256).astype(jnp.bfloat16)

    ret_count = [0]

    def give_back(ks):
        for k in ks:
            there = slot_of[minus((0, 0), offs[k])]
            for c in ((None,) if k == 0 else (0, 1)):
                dst_core = 1 - core if c is None else c
                cp = pltpu.make_async_remote_copy(
                    src_ref=y_buf.at[k * 2 + dst_core], dst_ref=back.at[there * 2 + core],
                    send_sem=ret_send.at[ret_count[0]], recv_sem=ret_recv.at[there * 2 + core],
                    device_id={"ep": device_at(offs[k], dst_core)}, device_id_type=MESH)
                cp.start()
                ret_count[0] += 1
                sends.append(cp)

    near, far = list(range(half)), list(range(half, n_chips))
    ready(near)
    gather_rows(0)
    for e in range(n_exp):
        w_copies[e * 3].wait()
        w_copies[e * 3 + 1].wait()
        gate_up(e)
        if e == 0:
            hop3()
    for e in range(n_exp):
        w_copies[e * 3 + 2].wait()
    hop4()
    down(0)
    own = pltpu.make_async_copy(y_buf.at[core], back.at[core], local_sem)
    own.start()
    give_back(near[::-1])

    ready(far)
    gather_rows(half)

    def far_gate_up(e, carry):
        gate_up(e)
        return carry

    lax.fori_loop(0, n_exp, far_gate_up, 0)
    down(half)
    give_back(far[::-1])

    sh_acc[...] = jnp.zeros_like(sh_acc)

    def shared_step(i, carry):
        slot = lax.rem(i, n_ring)
        for cp in ring_copies(i, slot):
            cp.wait()
        g = jnp.dot(h_ref[...], ring_g[slot], preferred_element_type=jnp.float32)
        u = jnp.dot(h_ref[...], ring_u[slot], preferred_element_type=jnp.float32)
        a = (jax.nn.silu(g) * u).astype(jnp.bfloat16)
        sh_acc[...] += jnp.dot(a, ring_d[slot], preferred_element_type=jnp.float32)

        @pl.when(i + n_ring < n_steps)
        def _():
            for cp in ring_copies(i + n_ring, slot):
                cp.start()

        return carry

    lax.fori_loop(0, n_steps, shared_step, 0)

    gates = gate_ref[...]
    g0 = gates.astype(jnp.bfloat16)
    rest = gates - g0.astype(jnp.float32)
    g1 = rest.astype(jnp.bfloat16)
    g2 = (rest - g1.astype(jnp.float32)).astype(jnp.bfloat16)
    gates3 = jnp.concatenate([g0, g1, g2], axis=0)
    own.wait()
    for k in range(n_chips):
        for c in ((1 - core,) if k == 0 else (0, 1)):
            pltpu.make_async_remote_copy(
                src_ref=y_buf.at[0], dst_ref=back.at[k * 2 + c], send_sem=ret_send.at[0],
                recv_sem=ret_recv.at[k * 2 + c], device_id={"ep": partner}, device_id_type=MESH).wait_recv()
    n_slot = n_chips * 2 * n_exp * SLOTS_EXP
    for j in range(hidden // 256):
        cs = slice(j * 256, (j + 1) * 256)
        part = jnp.dot(gates3, back[:, :, cs].reshape(n_slot, 256), preferred_element_type=jnp.float32)
        routed = part[:seqs] + part[seqs:2 * seqs] + part[2 * seqs:]
        shared = sh_acc[:, cs].astype(jnp.bfloat16).astype(jnp.float32)
        out_ref[:, cs] = (h_ref[:, cs].astype(jnp.float32) + shared + routed).astype(jnp.bfloat16)
    for cp in sends:
        cp.wait_send()


def slot_tables(routes, route_gates, n_dev, local_exp, top_slots):
    side = int((n_dev // 2) ** 0.5)
    offs = jnp.array(chip_order(side), jnp.int32)
    me = lax.axis_index("ep")
    core, my_x, my_y = me % 2, (me // 2) % side, me // (2 * side)
    chips = ((my_y + offs[:, 1]) % side) * side + (my_x + offs[:, 0]) % side
    devs = chips[:, None] * 2 + jnp.arange(2)[None, :]
    ids = devs[:, :, None] * local_exp + jnp.arange(local_exp)[None, None, :]
    ids = jnp.broadcast_to(ids[:, :, :, None], ids.shape + (top_slots,)).reshape(-1)
    pos = jnp.arange(ids.shape[0]) % top_slots
    seqs = routes.shape[0]
    hit = routes[None, :, :] == ids[:, None, None]
    has = jnp.any(hit, axis=2)
    earlier = jnp.arange(seqs)[:, None] < jnp.arange(seqs)[None, :]
    rank = jnp.dot(has.astype(jnp.bfloat16), earlier.astype(jnp.bfloat16), preferred_element_type=jnp.float32)
    sel = has & (rank == pos[:, None].astype(jnp.float32))
    gate = jnp.sum(jnp.where(hit & sel[:, :, None], route_gates[None, :, :], 0.0), axis=2).T
    wide = jnp.tile(sel, (1, LANES // seqs))
    lane_blk = jnp.arange(LANES) // seqs
    table = jnp.stack([wide & (lane_blk == 2 * v + core)[None, :] for v in range(2)]).astype(jnp.bfloat16)
    return table.reshape(2, n_dev, local_exp * top_slots, LANES), gate


def moe_call(n_dev, h_mid, table, gate, sh_gate, sh_up, sh_down, ex_gate, ex_up, ex_down):
    seqs, hidden = h_mid.shape
    n_exp, _, ff = ex_gate.shape
    n_chips = n_dev // 2
    n_src = n_chips
    slots = n_exp * SLOTS_EXP
    n_ring, blk = 4, 256
    bf = jnp.bfloat16
    dma = pltpu.SemaphoreType.DMA
    vmem = pl.BlockSpec(memory_space=pltpu.VMEM)
    hbm = pl.BlockSpec(memory_space=pl.ANY)
    return pl.pallas_call(
        functools.partial(moe_kernel, n_dev),
        out_shape=jax.ShapeDtypeStruct((seqs, hidden), bf),
        in_specs=[vmem] * 3 + [hbm] * 6,
        out_specs=vmem,
        scratch_shapes=[
            pltpu.VMEM((n_dev, seqs, hidden), bf),
            pltpu.VMEM((n_dev, slots, LANES), bf),
            pltpu.VMEM((n_exp, n_src * SLOTS_EXP, hidden), bf),
            pltpu.VMEM((n_exp, n_src * SLOTS_EXP, ff), bf),
            pltpu.VMEM((n_dev, slots, hidden), bf),
            pltpu.VMEM((n_dev, slots, hidden), bf),
            pltpu.VMEM((n_exp, hidden, ff), bf),
            pltpu.VMEM((n_exp, hidden, ff), bf),
            pltpu.VMEM((n_exp, ff, hidden), bf),
            pltpu.VMEM((n_ring, hidden, blk), bf),
            pltpu.VMEM((n_ring, hidden, blk), bf),
            pltpu.VMEM((n_ring, blk, hidden), bf),
            pltpu.VMEM((seqs, hidden), jnp.float32),
            dma((64,)), dma((64,)), dma((2 * n_chips,)), dma((2 * n_chips,)),
            dma((n_dev,)), dma((n_dev,)), dma((n_dev,)), dma((n_dev,)),
            dma((n_exp * 3,)), dma((3, n_ring)), dma,
        ],
        compiler_params=pltpu.CompilerParams(collective_id=0, has_side_effects=True, vmem_limit_bytes=67043328),
    )(h_mid, table, gate, sh_gate, sh_up, sh_down, ex_gate, ex_up, ex_down)


def solution(mesh):
    group_size = mesh.shape["ep"]

    def device_step(x_blk, cache_blk, len_blk, routes, route_gates, w_q, w_dkv, w_uk, w_uv, w_o, sh_gate, sh_up, sh_down, ex_gate, ex_up, ex_down):
        h_mid, kv_row = attend_local(x_blk, cache_blk, len_blk, w_q, w_dkv, w_uk, w_uv, w_o)
        table, gate = slot_tables(routes, route_gates, group_size, ex_gate.shape[0], SLOTS_EXP)
        layer_out = moe_call(group_size, h_mid, table, gate, sh_gate, sh_up, sh_down, ex_gate, ex_up, ex_down)
        return layer_out, kv_row

    batch_spec = P(("dp", "ep"))
    weight_spec = P()
    expert_spec = P("ep")
    in_specs = (batch_spec,) * 5 + (weight_spec,) * 8 + (expert_spec,) * 3
    return jax.shard_map(device_step, mesh=mesh, in_specs=in_specs, out_specs=(batch_spec, batch_spec), check_vma=False)
```

time: 142 us -> 96.4 us (0.68)
  Pallas kernels: 0 us -> 66.4 us
  matrix products: 63.3 us -> 21.4 us
  blocking collectives: 38.7 us -> 0 us
  waiting for transfers between devices: 19.9 us -> 0 us
  local copies, waits for them, and re-layouts: 10.1 us -> 3.81 us
  starting transfers between devices: 4.02 us -> 0 us
    pallas_call x0 -> x1, Pallas kernels: none -> 66.4 us  [moe_call(): pl.pallas_call(functools.partial(moe_kernel, n_dev), out_shape=jax.ShapeD...]
    all_to_all x1 -> x0, blocking collectives: 38.7 us -> none  [device_step(): recv_buf = lax.all_to_all(send_buf, 'ep', 1, 1, tiled=True)]
    dot_general x5 -> x1, matrix products: 38 us -> 0.2 us  [slot_tables(): jnp.dot(has.astype(jnp.bfloat16), earlier.astype(jnp.bfloat16), preferred...]
    all_to_all x1 -> x0, waiting for transfers between devices: 19.9 us -> none  [device_step(): lax.all_to_all(exp_out.reshape(local_exp, group_size, exp_cap, hidden), '...]
    all_to_all x1 -> x0, starting transfers between devices: 4.02 us -> none  [device_step(): lax.all_to_all(exp_out.reshape(local_exp, group_size, exp_cap, hidden), '...]
    gather x3 -> x0, local copies, waits for them, and re-layouts: 3.88 us -> none  [the longest x1 2.47 us: device_step(): jnp.take(h_mid, slot_token, axis=0)]
    dot_general x1, matrix products: 4.93 us -> 2.23 us  [attend_local(): jnp.dot(v_head.reshape(num_seq, num_heads * v_dim), w_o, preferred_elemen...]
    unnamed x34 -> x29, local copies, waits for them, and re-layouts: 0.6 us -> 2.49 us
  transfers between devices with their start and end apart: 1 -> 0, of which waited for: 1 -> 0; matrix products, arithmetic and copies ran while one was open for 5% -> 0% of each run, Pallas kernels for 0% -> 0%
where the time goes in v1:
time: 96.4 us; the launch traced here: 96.2 us
  Pallas kernels  66.4 us (69%)
  matrix products  21.4 us (22%)
  local copies, waits for them, and re-layouts  3.81 us (4%)
  other arithmetic  3.66 us (4%)
  between operations  0.98 us (1%)
    pallas_call x1, Pallas kernels, moe_call(): pl.pallas_call(functools.partial(moe_kernel, n_dev), out_shape=jax.ShapeD...  66.4 us
    dot_general x1, matrix products, attend_local(): jnp.dot(x_blk, w_q, preferred_element_type=jnp.float32).astype(jnp.bfloat16)  7.05 us
    dot_general x1, matrix products, attend_local(): jnp.einsum('bhc,blc->bhl', q_cat, cache_blk, preferred_element_type=jnp.f...  5.46 us
    dot_general x1, matrix products, attend_local(): jnp.einsum('bhl,blc->bhc', p_old, cache_blk, preferred_element_type=jnp.f...  2.56 us
    dot_general x1, matrix products, attend_local(): kv_raw = jnp.dot(x_blk, w_dkv, preferred_element_type=jnp.float32)  2.52 us
    unnamed x29, local copies, waits for them, and re-layouts  2.49 us
    dot_general x1, matrix products, attend_local(): jnp.dot(v_head.reshape(num_seq, num_heads * v_dim), w_o, preferred_elemen...  2.23 us

profile of v1, /device:TPU:97, one launch (start us, length us, event | category | flops | bytes accessed | tf_op | source)
XLA Modules:
  0.0 96.2 jit_solution(5058770653348283220)
XLA Ops:
  0.6 2.5 %fusion.33 = f32[32,576]{1,0:T(8,128)S(1)} fusion(bf16[32,2048]{1,0:T(8,128)(2,1)} %param.17, bf16[2048,576]{0,1:T(8,128)(2,1)} %param.23), kind=kOutput, calls=%fused_computation.80 | convolution fusion | flops 75497472 | bytes 2564096 | tf_op jit(solution)/shard_map/dot_general | solution.py:34
  3.1 0.7 convert_element_type.75
  3.8 0.1 subtract_convert_fusion.1
  4.0 7.0 %convolution_convert_fusion = bf16[32,3072]{1,0:T(8,128)(2,1)S(1)} fusion(bf16[32,2048]{1,0:T(8,128)(2,1)} %param.17, bf16[2048,3072]{1,0:T(8,128)(2,1)} %param.22), kind=kOutput, calls=%fused_computation | convolution fusion | flops 402751488 | bytes 12910592 | tf_op jit(solution)/shard_map/dot_general | solution.py:33
  11.1 0.3 reshape.229
  11.4 0.1 subtract_convert_fusion
  11.6 0.4 fusion.3
  12.0 0.1 pad_maximum_fusion
  12.2 0.1 fusion.44
  12.3 0.4 fusion.8
  12.6 0.1 iota_compare_fusion
  12.7 5.5 %fusion.32 = (f32[32,16]{1,0:T(8,128)S(1)}, f32[32,16,256]{2,1,0:T(8,128)S(1)}) fusion(bf16[32,256,576]{1,2,0:T(8,128)(2,1)} %param.18, bf16[32,16,576]{2,0,1:T(8,128)(2,1)S(1)} %pad_maximum_fusion, pred[32,256]{1,0:T(8,128)(4,1)S(1)} %iota_compare_fusion), kind=kOutput, calls=%fused_computation.79 | convolution fusion | flops 151387648 | bytes 10561536 | tf_op jit(solution)/shard_map/bhc,blc->bhl/dot_general | solution.py:41
  18.2 0.2 fusion.12
  18.5 0.2 slice-done.2
  18.7 2.6 %fusion.13 = f32[32,16,576]{2,1,0:T(8,128)S(1)} fusion(bf16[32,256,576]{1,2,0:T(8,128)(2,1)S(1)} %bitcast.26, f32[32,16,256]{2,1,0:T(8,128)S(1)} %get-tuple-element.13, f32[32,16]{1,0:T(8,128)S(1)} %get-tuple-element.9, f32[32,16]{1,0:T(8,128)S(1)} %multiply_maximum_fusion), kind=kOutput, calls=%fused_computation.27 | convolution fusion | flops 151388160 | bytes 11145216 | tf_op jit(solution)/shard_map/bhl,blc->bhc/dot_general | solution.py:51
  21.3 0.1 pad_maximum_fusion.1
  21.4 0.6 copy-done.3
  22.0 0.2 fusion.7
  22.2 0.6 fusion.5
  22.9 2.2 %fusion.2.h_ref = bf16[32,2048]{1,0:T(8,128)(2,1)} fusion(bf16[2048,2048]{1,0:T(8,128)(2,1)S(1)} %bitcast.28, bf16[32,2048]{1,0:T(8,128)(2,1)S(1)} %copy-done.2, bf16[16,4,8,128]{3,2,1,0:T(8,128)(2,1)S(1)} %fusion.5), kind=kOutput, calls=%fused_computation.4 | convolution fusion | flops 268763136 | bytes 8781824 | tf_op jit(solution)/shard_map/dot_general | solution.py:54
  25.2 0.1 iota_add_fusion
  25.3 0.1 broadcast_in_dim.24
  25.4 0.1 eq.52
  25.5 0.1 compare_reduce_fusion
  25.6 0.2 fusion.6
  25.9 0.2 copy.41
  26.0 0.2 tile.4
  26.3 0.3 tile.10
  26.7 0.8 add_convert_fusion.oh_ref
  27.5 0.8 select_reduce_fusion
  28.2 66.4 %shard_map.176 = bf16[32,2048]{1,0:T(8,128)(2,1)} custom-call(bf16[32,2048]{1,0:T(8,128)(2,1)} %fusion.2.h_ref, bf16[2,32,16,128]{3,2,1,0:T(8,128)(2,1)} %add_convert_fusion.oh_ref, f32[32,512]{1,0:T(8,128)} %bitcast.29, bf16[2048,2816]{1,0:T(8,128)(2,1)} %shg_hbm.1, bf16[2048,2816]{1,0:T(8,128)(2,1)} %shu_hbm.1, bf16[2816,2048]{1,0:T(8,128)(2,1)} %shd_hbm.1, ...), custom_call_target="tpu_custom_call" | custom-call | tf_op jit(solution)/shard_map/pallas_call | solution.py:416
  94.6 1.6 %copy.65 = bf16[32,2048]{1,0:T(8,128)(2,1)} copy(bf16[32,2048]{1,0:T(8,128)(2,1)} %shard_map.176) | data formatting | bytes 262144
  (41 shorter events, 0.4 us)
Async XLA Ops:
  4.0 7.6 %copy-start = (bf16[16,128,512]{2,1,0:T(8,128)(2,1)S(1)}, bf16[16,128,512]{2,1,0:T(8,128)(2,1)}, u32[]{:S(2)}) copy-start(bf16[16,128,512]{2,1,0:T(8,128)(2,1)} %param.24) | copy-start | bytes 6291460
  4.0 8.6 %copy-start.6 = (s32[32]{0:T(128)S(1)}, s32[32]{0:T(128)}, u32[]{:S(2)}) copy-start(s32[32]{0:T(128)} %param.19) | copy-start | bytes 388
  12.3 6.2 %slice-start = ((s8[9437184]{0:T(1024)(128)(4,1)}), s8[4194304]{0:T(1024)(128)(4,1)S(1)}, s32[]{:S(2)}) async-start(s8[9437184]{0:T(1024)(128)(4,1)} %bitcast.25), calls=%async_computation | async-start | bytes 8388608
  12.7 5.8 %slice-start.1 = ((s8[9437184]{0:T(1024)(128)(4,1)}), s8[4194304]{0:T(1024)(128)(4,1)S(1)}, s32[]{:S(2)}) async-start(s8[9437184]{0:T(1024)(128)(4,1)} %bitcast.25), calls=%async_computation.1 | async-start | bytes 8388608
  12.7 6.0 %slice-start.2 = ((s8[9437184]{0:T(1024)(128)(4,1)}), s8[1048576]{0:T(1024)(128)(4,1)S(1)}, s32[]{:S(2)}) async-start(s8[9437184]{0:T(1024)(128)(4,1)} %bitcast.25), calls=%async_computation.2 | async-start | bytes 2097152
  18.2 4.0 %copy-start.1 = (bf16[16,512,128]{2,1,0:T(8,128)(2,1)S(1)}, bf16[16,512,128]{2,1,0:T(8,128)(2,1)}, u32[]{:S(2)}) copy-start(bf16[16,512,128]{2,1,0:T(8,128)(2,1)} %param.25) | copy-start | bytes 6291460
  18.2 4.6 %slice-start.3 = ((s8[8388608]{0:T(1024)(128)(4,1)}), s8[4194304]{0:T(1024)(128)(4,1)S(1)}, s32[]{:S(2)}) async-start(s8[8388608]{0:T(1024)(128)(4,1)} %bitcast.27), calls=%async_computation.3 | async-start | bytes 8388608
  18.2 4.6 %copy-start.2 = (bf16[32,2048]{1,0:T(8,128)(2,1)S(1)}, bf16[32,2048]{1,0:T(8,128)(2,1)}, u32[]{:S(2)}) copy-start(bf16[32,2048]{1,0:T(8,128)(2,1)} %param.17) | copy-start | bytes 393220
  18.7 4.1 %slice-start.4 = ((s8[8388608]{0:T(1024)(128)(4,1)}), s8[4194304]{0:T(1024)(128)(4,1)S(1)}, s32[]{:S(2)}) async-start(s8[8388608]{0:T(1024)(128)(4,1)} %bitcast.27), calls=%async_computation.4 | async-start | bytes 8388608
  21.4 0.6 copy-start.3
  22.8 2.3 %copy-start.7 = (s32[16,1]{0,1:T(1,128)S(1)}, s32[16,1]{0,1:T(1,128)}, u32[]{:S(2)}) copy-start(s32[16,1]{0,1:T(1,128)} %constant.111) | copy-start | bytes 196
  22.8 2.3 %copy-start.8 = (s32[16,1]{0,1:T(1,128)S(1)}, s32[16,1]{0,1:T(1,128)}, u32[]{:S(2)}) copy-start(s32[16,1]{0,1:T(1,128)} %constant.112) | copy-start | bytes 196
  22.9 2.6 %copy-start.4 = (s32[32,6]{0,1:T(8,128)S(1)}, s32[32,6]{0,1:T(8,128)}, u32[]{:S(2)}) copy-start(s32[32,6]{0,1:T(8,128)} %param.20) | copy-start | bytes 2308
  22.9 4.6 %copy-start.5 = (f32[32,6]{0,1:T(8,128)S(1)}, f32[32,6]{0,1:T(8,128)}, u32[]{:S(2)}) copy-start(f32[32,6]{0,1:T(8,128)} %param.21) | copy-start | bytes 2308

commit v2 on v1

--- a/solution.py
+++ b/solution.py
@@ -11,49 +11,141 @@
 SLOTS_EXP = 8
 LANES = 128
 
-def rotary(vec, cos_t, sin_t):
-    half_dim = vec.shape[-1] // 2
-    lead_part = vec[..., :half_dim]
-    tail_part = vec[..., half_dim:]
-    return jnp.concatenate([lead_part * cos_t - tail_part * sin_t, tail_part * cos_t + lead_part * sin_t], axis=-1)
-
-
-def rotary_table(positions, rot_width):
-    half_dim = rot_width // 2
-    inv_freq = jnp.exp(jnp.arange(half_dim, dtype=jnp.float32) * (-2.0 * jnp.log(10000.0) / rot_width))
-    angle_val = positions.astype(jnp.float32)[:, None] * inv_freq[None, :]
-    return jnp.cos(angle_val), jnp.sin(angle_val)
-
-
-def attend_local(x_blk, cache_blk, len_blk, w_q, w_dkv, w_uk, w_uv, w_o):
-    num_seq = x_blk.shape[0]
-    num_heads, nope_dim, latent = w_uk.shape
-    rope_dim = cache_blk.shape[2] - latent
-    v_dim = w_uv.shape[2]
-    q_all = jnp.dot(x_blk, w_q, preferred_element_type=jnp.float32).astype(jnp.bfloat16).reshape(num_seq, num_heads, nope_dim + rope_dim)
-    kv_raw = jnp.dot(x_blk, w_dkv, preferred_element_type=jnp.float32)
-    cos_t, sin_t = rotary_table(len_blk, rope_dim)
-    kv_row = jnp.concatenate([kv_raw[:, :latent], rotary(kv_raw[:, latent:], cos_t, sin_t)], axis=1).astype(jnp.bfloat16)
-    q_rope = rotary(q_all[:, :, nope_dim:].astype(jnp.float32), cos_t[:, None, :], sin_t[:, None, :]).astype(jnp.bfloat16)
-    q_lat = jnp.einsum("bhn,hnc->bhc", q_all[:, :, :nope_dim], w_uk, preferred_element_type=jnp.float32).astype(jnp.bfloat16)
-    q_cat = jnp.concatenate([q_lat, q_rope], axis=2)
-    score_scale = (nope_dim + rope_dim) ** -0.5
-    s_old = jnp.einsum("bhc,blc->bhl", q_cat, cache_blk, preferred_element_type=jnp.float32) * score_scale
-    s_new = jnp.einsum("bhc,bc->bh", q_cat, kv_row, preferred_element_type=jnp.float32) * score_scale
-    valid_mask = jnp.arange(cache_blk.shape[1])[None, None, :] < len_blk[:, None, None]
-    s_old = jnp.where(valid_mask, s_old, -jnp.inf)
-    top_score = jnp.maximum(jnp.max(s_old, axis=2), s_new)
-    e_old = jnp.exp(s_old - top_score[:, :, None])
-    e_new = jnp.exp(s_new - top_score)
-    denom_sum = jnp.sum(e_old, axis=2) + e_new
-    p_old = (e_old / denom_sum[:, :, None]).astype(jnp.bfloat16)
-    p_new = (e_new / denom_sum).astype(jnp.bfloat16)
-    o_full = jnp.einsum("bhl,blc->bhc", p_old, cache_blk, preferred_element_type=jnp.float32) + p_new.astype(jnp.float32)[:, :, None] * kv_row.astype(jnp.float32)[:, None, :]
-    o_lat = o_full[:, :, :latent].astype(jnp.bfloat16)
-    v_head = jnp.einsum("bhc,hcv->bhv", o_lat, w_uv, preferred_element_type=jnp.float32).astype(jnp.bfloat16)
-    attn_out = jnp.dot(v_head.reshape(num_seq, num_heads * v_dim), w_o, preferred_element_type=jnp.float32).astype(jnp.bfloat16)
-    h_mid = (x_blk.astype(jnp.float32) + attn_out.astype(jnp.float32)).astype(jnp.bfloat16)
-    return h_mid, kv_row
+def attention(x_ref, lens_ref, cache_hbm, wq_hbm, wdkv_hbm, wuk_hbm, wuv_hbm, wo_hbm, kv_ref, h_out,
+              wq, wdkv, wuk, wuv, wo, cache, q_rows, kv_rows, o_rows, v_rows, a_sem, c_sem, while_loading):
+    seqs, hidden = x_ref.shape
+    heads, nope, latent = wuk.shape
+    rope = wdkv.shape[0] - latent
+    v_dim = wuv.shape[2]
+    pair = 2 * (nope + rope)
+    n_q = 4
+    q_blk = wq.shape[1] // n_q
+    c_blk = seqs // c_sem.shape[0]
+    copies = {}
+
+    def fetch(name, src, dst):
+        cp = pltpu.make_async_copy(src, dst, a_sem.at[len(copies)])
+        cp.start()
+        copies[name] = cp
+
+    fetch("dkv", wdkv_hbm, wdkv)
+    for i in range(n_q):
+        fetch(i, wq_hbm.at[:, i * q_blk:(i + 1) * q_blk], wq.at[:, i * q_blk:(i + 1) * q_blk])
+        if i == 0:
+            fetch("uk", wuk_hbm, wuk)
+
+    def cache_copy(i):
+        rows_b = pl.ds(i * c_blk, c_blk)
+        return pltpu.make_async_copy(cache_hbm.at[rows_b], cache.at[rows_b], c_sem.at[i])
+
+    for i in range(seqs // c_blk):
+        cache_copy(i).start()
+    fetch("uv", wuv_hbm, wuv)
+    fetch("o", wo_hbm, wo)
+
+    while_loading()
+    lane = lax.broadcasted_iota(jnp.int32, (seqs, rope), 1)
+    freq = jnp.exp(lax.rem(lane, rope // 2).astype(jnp.float32) * (-2.0 * jnp.log(10000.0) / rope))
+    row = lax.broadcasted_iota(jnp.int32, (seqs, rope), 0)
+    pos = jnp.zeros((seqs, rope), jnp.int32)
+    for b in range(seqs):
+        pos = jnp.where(row == b, lens_ref[b], pos)
+    angle = pos.astype(jnp.float32) * freq
+    cos_t = jnp.cos(angle)
+    sin_t = jnp.where(lane < rope // 2, -jnp.sin(angle), jnp.sin(angle))
+
+    def rotate(u):
+        swapped = jnp.concatenate([u[:, rope // 2:], u[:, :rope // 2]], axis=1)
+        return u * cos_t + swapped * sin_t
+
+    contract_last = (((1,), (1,)), ((), ()))
+    x = x_ref[...]
+    copies["dkv"].wait()
+    raw = lax.dot_general(x, wdkv[...], contract_last, preferred_element_type=jnp.float32)
+    lat = raw[:, :latent].astype(jnp.bfloat16)
+    pe = rotate(raw[:, latent:latent + rope]).astype(jnp.bfloat16)
+    kv_ref[:, :latent] = lat
+    kv_ref[:, latent:latent + rope] = pe
+    kv_rows[:, :latent] = lat.astype(jnp.float32)
+    kv_rows[:, latent:latent + rope] = pe.astype(jnp.float32)
+
+    n_lat = latent // LANES
+    for p in range(heads // 2):
+        if (p * pair) % q_blk == 0:
+            copies[p * pair // q_blk].wait()
+        if p == 0:
+            copies["uk"].wait()
+        qp = jnp.dot(x, wq[:, p * pair:(p + 1) * pair], preferred_element_type=jnp.float32).astype(jnp.bfloat16).astype(jnp.float32)
+        for i in range(2):
+            h = 2 * p + i
+            base = i * (nope + rope)
+            q_n = qp[:, base:base + nope].astype(jnp.bfloat16)
+            q_lat = jnp.dot(q_n, wuk[h], preferred_element_type=jnp.float32)
+            q_pe = rotate(qp[:, base + nope:base + nope + rope])
+            q_lat = q_lat.astype(jnp.bfloat16).astype(jnp.float32)
+            for t in range(n_lat):
+                q_rows[t, h * seqs:(h + 1) * seqs, :] = q_lat[:, t * LANES:(t + 1) * LANES]
+            q_rows[n_lat, h * seqs:(h + 1) * seqs, :rope] = q_pe.astype(jnp.bfloat16).astype(jnp.float32)
+
+    scale = (nope + rope) ** -0.5
+    keys = cache.shape[2]
+    key_id = lax.broadcasted_iota(jnp.int32, (heads, keys), 1)
+
+    def attend(i, carry):
+        cache_copy(i).wait()
+        ids = [i * c_blk + j for j in range(c_blk)]
+        qs = [[q_rows[t, pl.ds(b, heads, stride=seqs), :] for t in range(n_lat + 1)] for b in ids]
+        s_old, s_new, kls = [], [], []
+        for b, q in zip(ids, qs):
+            ql, qr = jnp.concatenate(q[:n_lat], axis=1), q[n_lat][:, :rope]
+            s_old.append(jnp.dot(ql.astype(jnp.bfloat16), cache[b, :latent, :], preferred_element_type=jnp.float32)
+                         + jnp.dot(qr.astype(jnp.bfloat16), cache[b, latent:latent + rope, :], preferred_element_type=jnp.float32))
+        for b, q in zip(ids, qs):
+            kv = kv_rows[pl.ds(b, 1), :]
+            prod = q[0] * kv[:, :LANES]
+            for t in range(1, n_lat):
+                prod += q[t] * kv[:, t * LANES:(t + 1) * LANES]
+            s_new.append(jnp.sum(prod, axis=1, keepdims=True)
+                         + jnp.sum(q[n_lat][:, :rope] * kv[:, latent:latent + rope], axis=1, keepdims=True))
+            kls.append(kv[:, :latent])
+        s_old = [jnp.where(key_id < lens_ref[b], s * scale, -jnp.inf) for b, s in zip(ids, s_old)]
+        s_old = jnp.concatenate(s_old, axis=0)
+        s_new = jnp.concatenate(s_new, axis=0) * scale
+        top = jnp.maximum(jnp.max(s_old, axis=1, keepdims=True), s_new)
+        e_old = jnp.exp(s_old - top)
+        e_new = jnp.exp(s_new - top)
+        total = jnp.sum(e_old, axis=1, keepdims=True) + e_new
+        p_old = (e_old / total).astype(jnp.bfloat16)
+        p_new = (e_new / total).astype(jnp.bfloat16).astype(jnp.float32)
+        for j, b in enumerate(ids):
+            hs = slice(j * heads, (j + 1) * heads)
+            o = lax.dot_general(p_old[hs], cache[b, :latent, :], contract_last, preferred_element_type=jnp.float32) + p_new[hs] * kls[j]
+            for t in range(n_lat):
+                o_rows[t, pl.ds(b, heads, stride=seqs), :] = o[:, t * LANES:(t + 1) * LANES]
+        return carry
+
+    lax.fori_loop(0, seqs // c_blk, attend, 0)
+
+    copies["uv"].wait()
+    for h in range(heads):
+        o = jnp.concatenate([o_rows[t, h * seqs:(h + 1) * seqs, :] for t in range(n_lat)], axis=1).astype(jnp.bfloat16)
+        v_rows[:, h * v_dim:(h + 1) * v_dim] = jnp.dot(o, wuv[h], preferred_element_type=jnp.float32).astype(jnp.bfloat16)
+    copies["o"].wait()
+    for j in range(hidden // 256):
+        cs = slice(j * 256, (j + 1) * 256)
+        a = jnp.dot(v_rows[...], wo[:, cs], preferred_element_type=jnp.float32).astype(jnp.bfloat16)
+        h_out[:, cs] = (x_ref[:, cs].astype(jnp.float32) + a.astype(jnp.float32)).astype(jnp.bfloat16)
+
+
+def attention_scratch(seqs, hidden, heads, nope, latent, rope, v_dim, keys):
+    bf = jnp.bfloat16
+    wide = latent + LANES
+    return [pltpu.VMEM((hidden, heads * (nope + rope)), bf), pltpu.VMEM((latent + rope, hidden), bf),
+            pltpu.VMEM((heads, nope, latent), bf), pltpu.VMEM((heads, latent, v_dim), bf),
+            pltpu.VMEM((heads * v_dim, hidden), bf), pltpu.VMEM((seqs, latent + rope, keys), bf),
+            pltpu.VMEM((wide // LANES, heads * seqs, LANES), jnp.float32), pltpu.VMEM((seqs, wide), jnp.float32),
+            pltpu.VMEM((latent // LANES, heads * seqs, LANES), jnp.float32), pltpu.VMEM((seqs, heads * v_dim), bf),
+            pltpu.SemaphoreType.DMA((8,)), pltpu.SemaphoreType.DMA((4,))]
 
 
 def chip_order(side):
@@ -64,9 +156,42 @@
     return sorted(offs, key=lambda off: (hops(off), -max(min(v, side - v) for v in off), off))
 
 
-def moe_kernel(n_dev, h_ref, oh_ref, gate_ref, shg_hbm, shu_hbm, shd_hbm, exg_hbm, exu_hbm, exd_hbm, out_ref,
-               h_all, oh_all, rows, act, y_buf, back, wg, wu, wd, ring_g, ring_u, ring_d, sh_acc,
-               ag_send, ag_recv, core_send, core_recv, oh_send_sem, oh_recv_sem, ret_send, ret_recv, w_sem, ring_sem, local_sem):
+def layer_kernel(n_dev, x_ref, lens_ref, routes_ref, gates_ref, cache_hbm, wq_hbm, wdkv_hbm, wuk_hbm, wuv_hbm, wo_hbm,
+                 shg_hbm, shu_hbm, shd_hbm, exg_hbm, exu_hbm, exd_hbm, out_ref, kv_ref,
+                 h_ref, oh_ref, gate_ref, h_all, oh_all, rows, act, y_buf, back, sh_acc,
+                 ag_send, ag_recv, core_send, core_recv, oh_send_sem, oh_recv_sem, ret_send, ret_recv, local_sem):
+    barrier = pltpu.get_barrier_semaphore()
+    me = lax.axis_index("ep")
+    for i in range(1, n_dev):
+        pl.semaphore_signal(barrier, inc=1, device_id={"ep": lax.rem(me + i, n_dev)}, device_id_type=MESH)
+
+    seqs, hidden = x_ref.shape
+    heads, nope, latent = wuk_hbm.shape
+
+    def attend(*scratch):
+        attention(x_ref, lens_ref, cache_hbm, wq_hbm, wdkv_hbm, wuk_hbm, wuv_hbm, wo_hbm, kv_ref, h_ref, *scratch,
+                  while_loading=lambda: slot_tables(n_dev, routes_ref, gates_ref, oh_ref, gate_ref))
+
+    pl.run_scoped(attend, *attention_scratch(seqs, hidden, heads, nope, latent, wdkv_hbm.shape[0] - latent, wuv_hbm.shape[2], cache_hbm.shape[2]))
+
+    def experts(*scratch):
+        moe(n_dev, h_ref, oh_ref, gate_ref, shg_hbm, shu_hbm, shd_hbm, exg_hbm, exu_hbm, exd_hbm, out_ref,
+            h_all, oh_all, rows, act, y_buf, back, *scratch[:-2], sh_acc,
+            ag_send, ag_recv, core_send, core_recv, oh_send_sem, oh_recv_sem, ret_send, ret_recv, *scratch[-2:], local_sem)
+
+    n_exp, _, ff = exg_hbm.shape
+    n_ring, blk = 4, 256
+    bf = jnp.bfloat16
+    pl.run_scoped(
+        experts,
+        pltpu.VMEM((n_exp, hidden, ff), bf), pltpu.VMEM((n_exp, hidden, ff), bf), pltpu.VMEM((n_exp, ff, hidden), bf),
+        pltpu.VMEM((n_ring, hidden, blk), bf), pltpu.VMEM((n_ring, hidden, blk), bf), pltpu.VMEM((n_ring, blk, hidden), bf),
+        pltpu.SemaphoreType.DMA((n_exp * 3,)), pltpu.SemaphoreType.DMA((3, n_ring)))
+
+
+def moe(n_dev, h_ref, oh_ref, gate_ref, shg_hbm, shu_hbm, shd_hbm, exg_hbm, exu_hbm, exd_hbm, out_ref,
+        h_all, oh_all, rows, act, y_buf, back, wg, wu, wd, ring_g, ring_u, ring_d, sh_acc,
+        ag_send, ag_recv, core_send, core_recv, oh_send_sem, oh_recv_sem, ret_send, ret_recv, w_sem, ring_sem, local_sem):
     side = int((n_dev // 2) ** 0.5)
     offs = chip_order(side)
     slot_of = {off: k for k, off in enumerate(offs)}
@@ -109,10 +234,7 @@
     h_all[core] = h_ref[...]
     oh_all[core] = oh_ref[0, core]
 
-    barrier = pltpu.get_barrier_semaphore()
-    for i in range(1, n_dev):
-        pl.semaphore_signal(barrier, inc=1, device_id={"ep": lax.rem(me + i, n_dev)}, device_id_type=MESH)
-    pl.semaphore_wait(barrier, n_dev - 1)
+    pl.semaphore_wait(pltpu.get_barrier_semaphore(), n_dev - 1)
 
     A, B = (0, 2), (2, 2)
     A1, A0, B0, B1 = (0, 1), (1, 1), (2, 1), (3, 1)
@@ -259,19 +381,13 @@
     ff = wg.shape[2]
 
     def gather_rows(k0):
-        def body(g, carry):
+        for g in range(half // 2):
             s0 = k0 * 2 + g * 4
-            table = oh_all[pl.ds(s0, 4)].reshape(4 * 2 * SLOTS_EXP, LANES)
-            toks = h_all.at[pl.ds(s0, 4)]
-            for j in range(hidden // 512):
-                got = jnp.dot(table, toks[:, :, j * 512:(j + 1) * 512].reshape(4 * seqs, 512), preferred_element_type=jnp.float32)
-                got = got.reshape(4, n_exp, SLOTS_EXP, 512)
-                for e in range(n_exp):
-                    rows[e, pl.ds(pl.multiple_of(g * 4 * SLOTS_EXP, 4 * SLOTS_EXP), 4 * SLOTS_EXP), j * 512:(j + 1) * 512] = (
-                        got[:, e].reshape(4 * SLOTS_EXP, 512).astype(jnp.bfloat16))
-            return carry
-
-        lax.fori_loop(0, half // 2, body, 0)
+            table = oh_all[s0:s0 + 4].reshape(4 * 2 * SLOTS_EXP, LANES)
+            got = jnp.dot(table, h_all[s0:s0 + 4].reshape(4 * seqs, hidden), preferred_element_type=jnp.float32)
+            got = got.reshape(4, n_exp, SLOTS_EXP, hidden)
+            for e in range(n_exp):
+                rows[e, g * 4 * SLOTS_EXP:(g + 1) * 4 * SLOTS_EXP, :] = got[:, e].reshape(4 * SLOTS_EXP, hidden).astype(jnp.bfloat16)
 
     def gate_up(e):
         r = rows.at[e]
@@ -356,12 +472,6 @@
 
     lax.fori_loop(0, n_steps, shared_step, 0)
 
-    gates = gate_ref[...]
-    g0 = gates.astype(jnp.bfloat16)
-    rest = gates - g0.astype(jnp.float32)
-    g1 = rest.astype(jnp.bfloat16)
-    g2 = (rest - g1.astype(jnp.float32)).astype(jnp.bfloat16)
-    gates3 = jnp.concatenate([g0, g1, g2], axis=0)
     own.wait()
     for k in range(n_chips):
         for c in ((1 - core,) if k == 0 else (0, 1)):
@@ -371,82 +481,85 @@
     n_slot = n_chips * 2 * n_exp * SLOTS_EXP
     for j in range(hidden // 256):
         cs = slice(j * 256, (j + 1) * 256)
-        part = jnp.dot(gates3, back[:, :, cs].reshape(n_slot, 256), preferred_element_type=jnp.float32)
-        routed = part[:seqs] + part[seqs:2 * seqs] + part[2 * seqs:]
+        part = lax.dot_general(gate_ref[...], back[:, :, cs].reshape(n_slot, 256), (((0,), (0,)), ((), ())), preferred_element_type=jnp.float32)
+        routed = part[:seqs] + part[seqs:2 * seqs] + part[2 * seqs:3 * seqs]
         shared = sh_acc[:, cs].astype(jnp.bfloat16).astype(jnp.float32)
         out_ref[:, cs] = (h_ref[:, cs].astype(jnp.float32) + shared + routed).astype(jnp.bfloat16)
     for cp in sends:
         cp.wait_send()
 
 
-def slot_tables(routes, route_gates, n_dev, local_exp, top_slots):
+def slot_tables(n_dev, routes_ref, gates_ref, oh_ref, gate_ref):
     side = int((n_dev // 2) ** 0.5)
-    offs = jnp.array(chip_order(side), jnp.int32)
     me = lax.axis_index("ep")
-    core, my_x, my_y = me % 2, (me // 2) % side, me // (2 * side)
-    chips = ((my_y + offs[:, 1]) % side) * side + (my_x + offs[:, 0]) % side
-    devs = chips[:, None] * 2 + jnp.arange(2)[None, :]
-    ids = devs[:, :, None] * local_exp + jnp.arange(local_exp)[None, None, :]
-    ids = jnp.broadcast_to(ids[:, :, :, None], ids.shape + (top_slots,)).reshape(-1)
-    pos = jnp.arange(ids.shape[0]) % top_slots
-    seqs = routes.shape[0]
-    hit = routes[None, :, :] == ids[:, None, None]
-    has = jnp.any(hit, axis=2)
-    earlier = jnp.arange(seqs)[:, None] < jnp.arange(seqs)[None, :]
-    rank = jnp.dot(has.astype(jnp.bfloat16), earlier.astype(jnp.bfloat16), preferred_element_type=jnp.float32)
-    sel = has & (rank == pos[:, None].astype(jnp.float32))
-    gate = jnp.sum(jnp.where(hit & sel[:, :, None], route_gates[None, :, :], 0.0), axis=2).T
-    wide = jnp.tile(sel, (1, LANES // seqs))
-    lane_blk = jnp.arange(LANES) // seqs
-    table = jnp.stack([wide & (lane_blk == 2 * v + core)[None, :] for v in range(2)]).astype(jnp.bfloat16)
-    return table.reshape(2, n_dev, local_exp * top_slots, LANES), gate
-
-
-def moe_call(n_dev, h_mid, table, gate, sh_gate, sh_up, sh_down, ex_gate, ex_up, ex_down):
-    seqs, hidden = h_mid.shape
-    n_exp, _, ff = ex_gate.shape
-    n_chips = n_dev // 2
-    n_src = n_chips
-    slots = n_exp * SLOTS_EXP
-    n_ring, blk = 4, 256
-    bf = jnp.bfloat16
-    dma = pltpu.SemaphoreType.DMA
-    vmem = pl.BlockSpec(memory_space=pltpu.VMEM)
-    hbm = pl.BlockSpec(memory_space=pl.ANY)
-    return pl.pallas_call(
-        functools.partial(moe_kernel, n_dev),
-        out_shape=jax.ShapeDtypeStruct((seqs, hidden), bf),
-        in_specs=[vmem] * 3 + [hbm] * 6,
-        out_specs=vmem,
-        scratch_shapes=[
-            pltpu.VMEM((n_dev, seqs, hidden), bf),
-            pltpu.VMEM((n_dev, slots, LANES), bf),
-            pltpu.VMEM((n_exp, n_src * SLOTS_EXP, hidden), bf),
-            pltpu.VMEM((n_exp, n_src * SLOTS_EXP, ff), bf),
-            pltpu.VMEM((n_dev, slots, hidden), bf),
-            pltpu.VMEM((n_dev, slots, hidden), bf),
-            pltpu.VMEM((n_exp, hidden, ff), bf),
-            pltpu.VMEM((n_exp, hidden, ff), bf),
-            pltpu.VMEM((n_exp, ff, hidden), bf),
-            pltpu.VMEM((n_ring, hidden, blk), bf),
-            pltpu.VMEM((n_ring, hidden, blk), bf),
-            pltpu.VMEM((n_ring, blk, hidden), bf),
-            pltpu.VMEM((seqs, hidden), jnp.float32),
-            dma((64,)), dma((64,)), dma((2 * n_chips,)), dma((2 * n_chips,)),
-            dma((n_dev,)), dma((n_dev,)), dma((n_dev,)), dma((n_dev,)),
-            dma((n_exp * 3,)), dma((3, n_ring)), dma,
-        ],
-        compiler_params=pltpu.CompilerParams(collective_id=0, has_side_effects=True, vmem_limit_bytes=67043328),
-    )(h_mid, table, gate, sh_gate, sh_up, sh_down, ex_gate, ex_up, ex_down)
+    core, my_x, my_y = lax.rem(me, 2), lax.rem(me // 2, side), me // (2 * side)
+    top_k, seqs = routes_ref.shape
+    per_chip = oh_ref.shape[1] * oh_ref.shape[2] // (n_dev // 2)
+    row = lax.broadcasted_iota(jnp.int32, (per_chip, LANES), 0)
+    exp_chip = per_chip // SLOTS_EXP
+    ids = jnp.concatenate([
+        row // SLOTS_EXP + exp_chip * (lax.rem(my_y + dy, side) * side + lax.rem(my_x + dx, side))
+        for dx, dy in chip_order(side)], axis=0)
+    n_slot = ids.shape[0]
+    pos = lax.rem(lax.broadcasted_iota(jnp.int32, (n_slot, LANES), 0), SLOTS_EXP)
+    block = lax.broadcasted_iota(jnp.int32, (n_slot, LANES), 1) // seqs
+    routes = jnp.concatenate([routes_ref[...]] * (LANES // seqs), axis=1)
+    gates = jnp.concatenate([gates_ref[...]] * (LANES // seqs), axis=1)
+    has = jnp.zeros((n_slot, LANES), jnp.float32)
+    gate = jnp.zeros((n_slot, LANES), jnp.float32)
+    for k in range(top_k):
+        hit = ids == routes[k:k + 1, :]
+        has = jnp.where(hit, 1.0, has)
+        gate = jnp.where(hit, gates[k:k + 1, :], gate)
+    src = lax.broadcasted_iota(jnp.int32, (LANES, LANES), 0)
+    dst = lax.broadcasted_iota(jnp.int32, (LANES, LANES), 1)
+    earlier = jnp.where((src < dst) & (src // seqs == dst // seqs), 1.0, 0.0).astype(jnp.bfloat16)
+    rank = jnp.dot(has.astype(jnp.bfloat16), earlier, preferred_element_type=jnp.float32)
+    sel = jnp.where(rank == pos.astype(jnp.float32), has, 0.0)
+    for v in range(2):
+        oh_ref[v] = jnp.where(block == 2 * v + core, sel, 0.0).astype(jnp.bfloat16).reshape(oh_ref.shape[1:])
+    gate = gate * sel
+    g0 = gate.astype(jnp.bfloat16).astype(jnp.float32)
+    g1 = (gate - g0).astype(jnp.bfloat16).astype(jnp.float32)
+    g2 = gate - g0 - g1
+    gate_ref[...] = jnp.where(block == 0, g0, jnp.where(block == 1, g1, jnp.where(block == 2, g2, 0.0))).astype(jnp.bfloat16)
 
 
 def solution(mesh):
-    group_size = mesh.shape["ep"]
+    n_dev = mesh.shape["ep"]
 
     def device_step(x_blk, cache_blk, len_blk, routes, route_gates, w_q, w_dkv, w_uk, w_uv, w_o, sh_gate, sh_up, sh_down, ex_gate, ex_up, ex_down):
-        h_mid, kv_row = attend_local(x_blk, cache_blk, len_blk, w_q, w_dkv, w_uk, w_uv, w_o)
-        table, gate = slot_tables(routes, route_gates, group_size, ex_gate.shape[0], SLOTS_EXP)
-        layer_out = moe_call(group_size, h_mid, table, gate, sh_gate, sh_up, sh_down, ex_gate, ex_up, ex_down)
+        seqs, hidden = x_blk.shape
+        n_exp, _, ff = ex_gate.shape
+        n_chips = n_dev // 2
+        slots = n_exp * SLOTS_EXP
+        half_rows = n_chips * SLOTS_EXP
+        bf = jnp.bfloat16
+        dma = pltpu.SemaphoreType.DMA
+        vmem = pl.BlockSpec(memory_space=pltpu.VMEM)
+        hbm = pl.BlockSpec(memory_space=pl.ANY)
+        layer_out, kv_row = pl.pallas_call(
+            functools.partial(layer_kernel, n_dev),
+            out_shape=(jax.ShapeDtypeStruct((seqs, hidden), bf), jax.ShapeDtypeStruct((seqs, w_dkv.shape[1]), bf)),
+            in_specs=[vmem, pl.BlockSpec(memory_space=pltpu.SMEM), vmem, vmem] + [hbm] * 12,
+            out_specs=(vmem, vmem),
+            scratch_shapes=[
+                pltpu.VMEM((seqs, hidden), bf),
+                pltpu.VMEM((2, n_dev, slots, LANES), bf),
+                pltpu.VMEM((n_dev * slots, LANES), bf),
+                pltpu.VMEM((n_dev, seqs, hidden), bf),
+                pltpu.VMEM((n_dev, slots, LANES), bf),
+                pltpu.VMEM((n_exp, half_rows, hidden), bf),
+                pltpu.VMEM((n_exp, half_rows, ff), bf),
+                pltpu.VMEM((n_dev, slots, hidden), bf),
+                pltpu.VMEM((n_dev, slots, hidden), bf),
+                pltpu.VMEM((seqs, hidden), jnp.float32),
+                dma((64,)), dma((64,)), dma((2 * n_chips,)), dma((2 * n_chips,)),
+                dma((n_dev,)), dma((n_dev,)), dma((n_dev,)), dma((n_dev,)), dma,
+            ],
+            compiler_params=pltpu.CompilerParams(collective_id=0, has_side_effects=True, vmem_limit_bytes=67043328),
+        )(x_blk, len_blk, routes.T, route_gates.T, cache_blk.transpose(0, 2, 1), w_q, w_dkv.T, w_uk, w_uv, w_o,
+          sh_gate, sh_up, sh_down, ex_gate, ex_up, ex_down)
         return layer_out, kv_row
 
     batch_spec = P(("dp", "ep"))

time: 96.4 us -> 81.2 us (0.84); the launches traced: 96.2 us -> 79.9 us
  matrix products: 21.4 us -> 0 us
  Pallas kernels: 66.4 us -> 76.3 us
  other arithmetic: 3.66 us -> 0 us
    dot_general x9 -> x0, matrix products: 21.4 us -> none  [the longest x1 7.05 us: attend_local(): jnp.dot(x_blk, w_q, preferred_element_type=jnp.float32).astype(jnp.bfloat16)]
    pallas_call x1, Pallas kernels: 66.4 us -> 76.3 us  [device_step(): pl.pallas_call(functools.partial(layer_kernel, n_dev), out_shape=(jax.Sha...]
    convert_element_type x5 -> x0, other arithmetic: 1.48 us -> none  [the longest x1 0.75 us: slot_tables(): jnp.stack([wide & (lane_blk == 2 * v + core)[None, :] for v in range(2)])]
    reduce_sum x2 -> x0, other arithmetic: 1.01 us -> none  [the longest x1 0.76 us: slot_tables(): jnp.sum(jnp.where(hit & sel[:, :, None], route_gates[None, :, :], 0.0), a...]
    unnamed x29 -> x2, local copies, waits for them, and re-layouts: 2.49 us -> 2.97 us
where the time goes in v2:
time: 81.2 us; the launch traced here: 79.9 us
  Pallas kernels  76.3 us (94%)
  local copies, waits for them, and re-layouts  2.97 us (4%)
    pallas_call x1, Pallas kernels, device_step(): pl.pallas_call(functools.partial(layer_kernel, n_dev), out_shape=(jax.Sha...  76.3 us
    unnamed x2, local copies, waits for them, and re-layouts  2.97 us

profile of v2, /device:TPU:97, one launch (start us, length us, event | category | flops | bytes accessed | tf_op | source)
XLA Modules:
  0.0 79.9 jit_solution(28380328306349282)
XLA Ops:
  0.6 76.3 %shard_map.167 = (bf16[32,2048]{1,0:T(8,128)(2,1)}, bf16[32,576]{1,0:T(8,128)(2,1)}) custom-call(bf16[32,2048]{1,0:T(8,128)(2,1)} %x_ref.1, s32[32]{0:T(128)} %lens_ref.1, s32[6,32]{1,0:T(8,128)} %bitcast.6, f32[6,32]{1,0:T(8,128)} %bitcast.7, bf16[32,576,256]{2,1,0:T(8,128)(2,1)} %bitcast.4, bf16[2048,3072]{1,0:T(8,128)(2,1)} %wq_hbm.1, ...), custom_call_target="tpu_custom_call" | custom-call | tf_op jit(solution)/shard_map/pallas_call | solution.py:541
  76.9 1.6 %copy.20 = bf16[32,2048]{1,0:T(8,128)(2,1)} copy(bf16[32,2048]{1,0:T(8,128)(2,1)} %get-tuple-element.4) | data formatting | bytes 262144
  78.5 1.4 %copy.21 = bf16[32,576]{1,0:T(8,128)(2,1)} copy(bf16[32,576]{1,0:T(8,128)(2,1)} %get-tuple-element.5) | data formatting | bytes 73728

commit v3 on v2

--- a/solution.py
+++ b/solution.py
@@ -145,7 +145,7 @@
             pltpu.VMEM((heads * v_dim, hidden), bf), pltpu.VMEM((seqs, latent + rope, keys), bf),
             pltpu.VMEM((wide // LANES, heads * seqs, LANES), jnp.float32), pltpu.VMEM((seqs, wide), jnp.float32),
             pltpu.VMEM((latent // LANES, heads * seqs, LANES), jnp.float32), pltpu.VMEM((seqs, heads * v_dim), bf),
-            pltpu.SemaphoreType.DMA((8,)), pltpu.SemaphoreType.DMA((4,))]
+            pltpu.SemaphoreType.DMA((8,)), pltpu.SemaphoreType.DMA((2,))]
 
 
 def chip_order(side):
@@ -236,7 +236,7 @@
 
     pl.semaphore_wait(pltpu.get_barrier_semaphore(), n_dev - 1)
 
-    A, B = (0, 2), (2, 2)
+    A, B, WHOLE = (0, 2), (2, 2), (0, 4)
     A1, A0, B0, B1 = (0, 1), (1, 1), (2, 1), (3, 1)
     xp, xm, yp, ym = (1, 0), (side - 1, 0), (0, 1), (0, side - 1)
     pieces, sends, core_pieces = {}, [], {}
@@ -403,26 +403,32 @@
             both = jnp.dot(r[...], jnp.concatenate([wg[e, :, cs], wu[e, :, cs]], axis=1), preferred_element_type=jnp.float32)
             act[e, :, cs] = (jax.nn.silu(both[:, :wid]) * both[:, wid:]).astype(jnp.bfloat16)
 
-    def down(k0):
-        for j in range(hidden // 256):
+    def down(k0, part):
+        for j in range(part[0] * q4 // 256, (part[0] + part[1]) * q4 // 256):
             cs = slice(j * 256, (j + 1) * 256)
             outs = [jnp.dot(act[e], wd[e, :, cs], preferred_element_type=jnp.float32).reshape(n_src, 1, SLOTS_EXP, 256) for e in range(n_exp)]
             y_buf[k0 * 2:k0 * 2 + n_src, :, cs] = jnp.concatenate(outs, axis=1).reshape(n_src, n_exp * SLOTS_EXP, 256).astype(jnp.bfloat16)
 
     ret_count = [0]
 
-    def give_back(ks):
-        for k in ks:
-            there = slot_of[minus((0, 0), offs[k])]
-            for c in ((None,) if k == 0 else (0, 1)):
-                dst_core = 1 - core if c is None else c
-                cp = pltpu.make_async_remote_copy(
-                    src_ref=y_buf.at[k * 2 + dst_core], dst_ref=back.at[there * 2 + core],
-                    send_sem=ret_send.at[ret_count[0]], recv_sem=ret_recv.at[there * 2 + core],
-                    device_id={"ep": device_at(offs[k], dst_core)}, device_id_type=MESH)
-                cp.start()
-                ret_count[0] += 1
-                sends.append(cp)
+    def give_back(ks, parts):
+        for part in parts:
+            for k in ks:
+                back_k = slot_of[minus((0, 0), offs[k])]
+                k1, back_k1 = (back_k, k) if back_k in ks else (k, back_k)
+                place = k + core * (k1 - k)
+                there = back_k + core * (back_k1 - back_k)
+                off = tuple(offs[k][a] + core * (offs[k1][a] - offs[k][a]) for a in range(2))
+                for c in ((None,) if k == 0 else (0, 1)):
+                    dst_core = 1 - core if c is None else c
+                    cp = pltpu.make_async_remote_copy(
+                        src_ref=y_buf.at[place * 2 + dst_core, :, cols_of(part)],
+                        dst_ref=back.at[there * 2 + core, :, cols_of(part)],
+                        send_sem=ret_send.at[ret_count[0]], recv_sem=ret_recv.at[(there * 2 + core) * 2 + part[0] // 2],
+                        device_id={"ep": device_at(off, dst_core)}, device_id_type=MESH)
+                    cp.start()
+                    ret_count[0] += 1
+                    sends.append(cp)
 
     near, far = list(range(half)), list(range(half, n_chips))
     ready(near)
@@ -436,10 +442,10 @@
     for e in range(n_exp):
         w_copies[e * 3 + 2].wait()
     hop4()
-    down(0)
+    down(0, WHOLE)
     own = pltpu.make_async_copy(y_buf.at[core], back.at[core], local_sem)
     own.start()
-    give_back(near[::-1])
+    give_back(near[::-1], (WHOLE,))
 
     ready(far)
     gather_rows(half)
@@ -449,8 +455,9 @@
         return carry
 
     lax.fori_loop(0, n_exp, far_gate_up, 0)
-    down(half)
-    give_back(far[::-1])
+    for part in (A, B):
+        down(half, part)
+        give_back(far[::-1], (part,))
 
     sh_acc[...] = jnp.zeros_like(sh_acc)
 
@@ -473,13 +480,22 @@
     lax.fori_loop(0, n_steps, shared_step, 0)
 
     own.wait()
-    for k in range(n_chips):
+
+    def returned(k, part):
         for c in ((1 - core,) if k == 0 else (0, 1)):
             pltpu.make_async_remote_copy(
-                src_ref=y_buf.at[0], dst_ref=back.at[k * 2 + c], send_sem=ret_send.at[0],
-                recv_sem=ret_recv.at[k * 2 + c], device_id={"ep": partner}, device_id_type=MESH).wait_recv()
+                src_ref=y_buf.at[0, :, cols_of(part)], dst_ref=back.at[k * 2 + c, :, cols_of(part)], send_sem=ret_send.at[0],
+                recv_sem=ret_recv.at[(k * 2 + c) * 2 + part[0] // 2], device_id={"ep": partner}, device_id_type=MESH).wait_recv()
+
+    from_near = [slot_of[minus((0, 0), offs[k])] for k in near]
+    for k in from_near:
+        returned(k, WHOLE)
     n_slot = n_chips * 2 * n_exp * SLOTS_EXP
     for j in range(hidden // 256):
+        if j * 256 % (2 * q4) == 0:
+            for k in range(n_chips):
+                if k not in from_near:
+                    returned(k, A if j == 0 else B)
         cs = slice(j * 256, (j + 1) * 256)
         part = lax.dot_general(gate_ref[...], back[:, :, cs].reshape(n_slot, 256), (((0,), (0,)), ((), ())), preferred_element_type=jnp.float32)
         routed = part[:seqs] + part[seqs:2 * seqs] + part[2 * seqs:3 * seqs]
@@ -555,7 +571,7 @@
                 pltpu.VMEM((n_dev, slots, hidden), bf),
                 pltpu.VMEM((seqs, hidden), jnp.float32),
                 dma((64,)), dma((64,)), dma((2 * n_chips,)), dma((2 * n_chips,)),
-                dma((n_dev,)), dma((n_dev,)), dma((n_dev,)), dma((n_dev,)), dma,
+                dma((n_dev,)), dma((n_dev,)), dma((2 * n_dev,)), dma((2 * n_dev,)), dma,
             ],
             compiler_params=pltpu.CompilerParams(collective_id=0, has_side_effects=True, vmem_limit_bytes=67043328),
         )(x_blk, len_blk, routes.T, route_gates.T, cache_blk.transpose(0, 2, 1), w_q, w_dkv.T, w_uk, w_uv, w_o,

time: 81.2 us -> 78.9 us (0.972); the launches traced: 79.9 us -> 78.7 us
  Pallas kernels: 76.3 us -> 75.1 us
    pallas_call x1, Pallas kernels: 76.3 us -> 75.1 us  [device_step(): pl.pallas_call(functools.partial(layer_kernel, n_dev), out_shape=(jax.Sha...]
where the time goes in v3:
time: 78.9 us; the launch traced here: 78.7 us
  Pallas kernels  75.1 us (95%)
  local copies, waits for them, and re-layouts  2.97 us (4%)
    pallas_call x1, Pallas kernels, device_step(): pl.pallas_call(functools.partial(layer_kernel, n_dev), out_shape=(jax.Sha...  75.1 us
    unnamed x2, local copies, waits for them, and re-layouts  2.97 us

profile of v3, /device:TPU:97, one launch (start us, length us, event | category | flops | bytes accessed | tf_op | source)
XLA Modules:
  0.0 78.7 jit_solution(4075515414359708527)
XLA Ops:
  0.6 75.1 %shard_map.167 = (bf16[32,2048]{1,0:T(8,128)(2,1)}, bf16[32,576]{1,0:T(8,128)(2,1)}) custom-call(bf16[32,2048]{1,0:T(8,128)(2,1)} %x_ref.1, s32[32]{0:T(128)} %lens_ref.1, s32[6,32]{1,0:T(8,128)} %bitcast.6, f32[6,32]{1,0:T(8,128)} %bitcast.7, bf16[32,576,256]{2,1,0:T(8,128)(2,1)} %bitcast.4, bf16[2048,3072]{1,0:T(8,128)(2,1)} %wq_hbm.1, ...), custom_call_target="tpu_custom_call" | custom-call | tf_op jit(solution)/shard_map/pallas_call | solution.py:557
  75.7 1.6 %copy.20 = bf16[32,2048]{1,0:T(8,128)(2,1)} copy(bf16[32,2048]{1,0:T(8,128)(2,1)} %get-tuple-element.4) | data formatting | bytes 262144
  77.3 1.4 %copy.21 = bf16[32,576]{1,0:T(8,128)(2,1)} copy(bf16[32,576]{1,0:T(8,128)(2,1)} %get-tuple-element.5) | data formatting | bytes 73728

commit v4 on v3

--- a/solution.py
+++ b/solution.py
@@ -318,10 +318,12 @@
     arrived(x2, A0, A1)
     forward(x2, A, yp)
     forward(x2, A, ym)
+    forward(x2, A, y2)
     to_partner(x2, A)
     arrived(y2, B0, B1)
     forward(y2, B, xp)
     forward(y2, B, xm)
+    forward(y2, B, x2)
     to_partner(y2, B)
     diagonals = [(dx, dy) for dy in (1, side - 1) for dx in (1, side - 1)]
     for off in diagonals:
@@ -343,13 +345,11 @@
     to_partner(y2, A)
 
     def hop3():
-        for off, d, quarter in (((2, side - 1), yp, A0), ((2, 1), ym, A1)):
+        for off in ((2, side - 1), (2, 1)):
             arrived(off, A)
-            forward(off, quarter, d)
             to_partner(off, A)
-        for off, d, quarter in (((side - 1, 2), xp, B0), ((1, 2), xm, B1)):
+        for off in ((side - 1, 2), (1, 2)):
             arrived(off, B)
-            forward(off, quarter, d)
             to_partner(off, B)
         for off in ((2, side - 1), (2, 1)):
             arrived(off, B0, B1)
@@ -359,11 +359,9 @@
             to_partner(off, A)
 
     def hop4():
-        far = (2, 2)
-        arrived(far, A0, A1)
-        to_partner(far, A)
-        arrived(far, B0, B1)
-        to_partner(far, B)
+        for part in (A, B):
+            arrived((2, 2), part)
+            to_partner((2, 2), part)
 
     def ready(ks):
         for k in ks:

time: 78.9 us -> 76.6 us (0.971)
  Pallas kernels: 75.1 us -> 72.3 us
    pallas_call x1, Pallas kernels: 75.1 us -> 72.3 us  [device_step(): pl.pallas_call(functools.partial(layer_kernel, n_dev), out_shape=(jax.Sha...]
where the time goes in v4:
time: 76.6 us; the launch traced here: 75.9 us
  Pallas kernels  72.3 us (94%)
  local copies, waits for them, and re-layouts  2.97 us (4%)
    pallas_call x1, Pallas kernels, device_step(): pl.pallas_call(functools.partial(layer_kernel, n_dev), out_shape=(jax.Sha...  72.3 us
    unnamed x2, local copies, waits for them, and re-layouts  2.97 us

profile of v4, /device:TPU:97, one launch (start us, length us, event | category | flops | bytes accessed | tf_op | source)
XLA Modules:
  0.0 75.9 jit_solution(9720562199237980945)
XLA Ops:
  0.6 72.3 %shard_map.167 = (bf16[32,2048]{1,0:T(8,128)(2,1)}, bf16[32,576]{1,0:T(8,128)(2,1)}) custom-call(bf16[32,2048]{1,0:T(8,128)(2,1)} %x_ref.1, s32[32]{0:T(128)} %lens_ref.1, s32[6,32]{1,0:T(8,128)} %bitcast.6, f32[6,32]{1,0:T(8,128)} %bitcast.7, bf16[32,576,256]{2,1,0:T(8,128)(2,1)} %bitcast.4, bf16[2048,3072]{1,0:T(8,128)(2,1)} %wq_hbm.1, ...), custom_call_target="tpu_custom_call" | custom-call | tf_op jit(solution)/shard_map/pallas_call | solution.py:555
  72.9 1.6 %copy.20 = bf16[32,2048]{1,0:T(8,128)(2,1)} copy(bf16[32,2048]{1,0:T(8,128)(2,1)} %get-tuple-element.4) | data formatting | bytes 262144
  74.5 1.4 %copy.21 = bf16[32,576]{1,0:T(8,128)(2,1)} copy(bf16[32,576]{1,0:T(8,128)(2,1)} %get-tuple-element.5) | data formatting | bytes 73728
